TPU v7x, 32 devices: a whole 2x2x4 slice. The times are simulated.
32 devices in a mesh: gx: 2 (over y), gy: 4 (over x, core), gz: 4 (over z).
Axes of the slice: x: 2, y: 2, z: 4, core: 2. Of those that a mesh axis runs over, the one named last changes fastest.
Arguments:
- positions: float32 [3, 8, 16, 512], P(None, 'gx', 'gy', 'gz'), may hold values from 0 to 1
- charges: float32 [8, 16, 512], P('gx', 'gy', 'gz'), may hold values from -1.2 to 1.2
- counts: int32 [8, 16, 16], P('gx', 'gy', 'gz'), may hold values from 16 to 32
- moment_shift: bfloat16 [8, 81, 81], replicated, may hold values from -0.25 to 0.25
- far_operators: bfloat16 [81, 25600], replicated, may hold values from -0.046875 to 0.046875
- local_shift: bfloat16 [8, 81, 81], replicated, may hold values from -0.625 to 0.625
- lattice_operator: bfloat16 [81, 81], replicated, may hold values from -0.625 to 0.625
Outputs:
- potential: float32 [8, 16, 512], P('gx', 'gy', 'gz')
- electric_field: float32 [3, 8, 16, 512], P(None, 'gx', 'gy', 'gz')
Inputs may be any that keep to these rules, and one draw needn't show every extreme that they name: `counts`: number of live charges in each leaf; slots at or past it are pads.
All inputs are finite; a program needn't handle non-finite values.
Results may differ from a plain program's by a relative error of at most 0.00035.
Values sent between devices are 32-bit elements; how exact they have to be, the bound alone decides.
A program may use at most 256 MiB of HBM per device.

v0:
```python
import jax
import jax.numpy as jnp
import numpy as np
from jax import lax
from jax.experimental import pallas as pl
from jax.experimental.pallas import tpu as pltpu
from jax.sharding import PartitionSpec as P

ORDER = 8
SLOTS = 32


SOFTENING = 0.0625


def padded(cells, sides, width):
    for axis, dim in sides:
        count = lax.axis_size(axis)
        head = lax.slice_in_dim(cells, 0, width, axis=dim)
        tail = lax.slice_in_dim(cells, cells.shape[dim] - width, cells.shape[dim], axis=dim)
        cells = jnp.concatenate(
            [
                lax.ppermute(tail, axis, [(i, (i + 1) % count) for i in range(count)]),
                cells,
                lax.ppermute(head, axis, [((i + 1) % count, i) for i in range(count)]),
            ],
            axis=dim,
        )
    return cells


def offset_table():
    listed = []
    for shift_x in range(-3, 4):
        for shift_y in range(-3, 4):
            for shift_z in range(-3, 4):
                if max(abs(shift_x), abs(shift_y), abs(shift_z)) >= 2:
                    listed.append((shift_x, shift_y, shift_z))
    return np.array(listed, dtype=np.int32)


def exponent_table(degree):
    listed = []
    for accumulated in range(degree + 1):
        for height in (0, 1):
            for power_x in range(accumulated - height + 1):
                listed.append((power_x, accumulated - height - power_x, height))
    return np.array(listed, dtype=np.int32)


NT = (((1,), (1,)), ((), ()))
TN = (((0,), (0,)), ((), ()))
F32 = jnp.float32
BF16 = jnp.bfloat16
LANES = 128


def split_rows(data):
    upper = data.astype(BF16)
    lower = (data - upper.astype(F32)).astype(BF16)
    return upper, lower


def apply(data, operator):
    upper, lower = split_rows(data)
    return lax.dot_general(upper, operator, NT, preferred_element_type=F32) + lax.dot_general(
        lower, operator, NT, preferred_element_type=F32
    )


def exact(left, right, dims):
    return lax.dot_general(
        left, right, dims, precision=lax.Precision.HIGHEST, preferred_element_type=F32
    )


def permutation(block_x, block_y, block_z):
    half_x, half_y, half_z = (block_x // 2, block_y // 2, block_z // 2)
    number = block_x * block_y * block_z
    table = np.zeros((number, number), np.float32)
    for x in range(block_x):
        for y in range(block_y):
            for z in range(block_z):
                octant = 4 * (x % 2) + 2 * (y % 2) + z % 2
                parent = (x // 2 * half_y + y // 2) * half_z + z // 2
                table[octant * (number // 8) + parent, (x * block_y + y) * block_z + z] = 1.0
    return table


def powers_of(values):
    listed = [jnp.ones_like(values)]
    for exponent in range(ORDER):
        listed.append(listed[-1] * values)
    return listed


def monomial_map(powers_x, powers_y, centred_z):
    made = {}
    for power_x, power_y, power_z in exponent_table(ORDER):
        key = (int(power_x), int(power_y), int(power_z))
        if key[2] == 0:
            made[key] = powers_x[key[0]] * powers_y[key[1]]
        else:
            made[key] = made[(key[0], key[1], 0)] * centred_z
    return made


def cell_picker(rows, cells):
    row = lax.broadcasted_iota(jnp.int32, (rows, cells * SLOTS), 0)
    lane = lax.broadcasted_iota(jnp.int32, (rows, cells * SLOTS), 1)
    return (lane // SLOTS == row).astype(F32)


def halo_slices(move, block, halo):
    if move == 1:
        return pl.ds(block, halo), pl.ds(0, halo)
    if move == -1:
        return pl.ds(halo, halo), pl.ds(block + halo, halo)
    return pl.ds(halo, block), pl.ds(halo, block)


def halo_copies(window, block, halo, numbers, at, sends, receives):
    copies = []
    for count in range(27):
        moves = (count // 9 - 1, count // 3 % 3 - 1, count % 3 - 1)
        if moves == (0, 0, 0):
            continue
        target = tuple(
            lax.rem(at[axis] + moves[axis] + numbers[axis], numbers[axis]) for axis in range(3)
        )
        from_x, to_x = halo_slices(moves[0], block[0], halo)
        from_y, to_y = halo_slices(moves[1], block[1], halo)
        copies.append(
            pltpu.make_async_remote_copy(
                src_ref=window.at[1, from_x, from_y],
                dst_ref=window.at[1 - moves[2], to_x, to_y],
                send_sem=sends.at[count],
                recv_sem=receives.at[count],
                device_id=target,
                device_id_type=pl.DeviceIdType.MESH,
            )
        )
    return copies


def local_moments(sizes, data_ref, shift_ref, order_ref, table, leaf_flat, leaf_wide, mid_wide, own_upper):
    block_x, block_y, cells = sizes
    terms = shift_ref.shape[1]
    columns = data_ref.shape[1]
    padded_terms = table.shape[0] // columns - 1
    powers_x = powers_of(data_ref[0] - 0.5)
    powers_x = [value * data_ref[3] for value in powers_x]
    powers_y = powers_of(data_ref[1] - 0.5)
    made = monomial_map(powers_x, powers_y, data_ref[2] - 0.5)
    for row, key in enumerate(exponent_table(ORDER)):
        table[row * columns : (row + 1) * columns, :] = made[tuple(int(v) for v in key)]
    spare = (padded_terms + 1 - terms) * columns
    table[terms * columns :, :] = jnp.zeros((spare, table.shape[1]), F32)
    picker = cell_picker(8, cells)
    for column in range(columns):
        rows = table[pl.ds(column, padded_terms, stride=columns), :]
        found = exact(picker, rows, NT)[:cells]
        found = jnp.concatenate([found, jnp.zeros((cells, LANES - padded_terms), F32)], axis=1)
        leaf_flat[column * cells : (column + 1) * cells, :] = found
        leaf_wide[1, 2 + column // block_y, 2 + column % block_y] = found
    ordered = exact(order_ref[...], leaf_flat[...], (((1,), (0,)), ((), ())))
    parents = ordered.shape[0] // 8
    mid = jnp.zeros((parents, terms), F32)
    for octant in range(8):
        piece = ordered[octant * parents : (octant + 1) * parents, :terms]
        mid = mid + apply(piece, shift_ref[octant])
    spare_lanes = jnp.zeros((8, LANES - terms), F32)
    mids = jnp.concatenate([mid, spare_lanes], axis=1)
    half_y, half_z = block_y // 2, cells // 2
    for column in range(block_x // 2 * half_y):
        mid_wide[1, 2 + column // half_y, 2 + column % half_y] = mids[
            column * half_z : (column + 1) * half_z
        ]
    up = jnp.zeros((8, terms), F32)
    for octant in range(8):
        piece = jnp.broadcast_to(mid[octant : octant + 1], (8, terms))
        up = up + apply(piece, shift_ref[octant])
    own_upper[...] = jnp.concatenate([up, spare_lanes], axis=1)


def field_kernel(
    sizes,
    numbers,
    plan_ref,
    where_ref,
    own_ref,
    data_ref,
    live_ref,
    shift_ref,
    far_ref,
    down_ref,
    lattice_ref,
    order_ref,
    merge_ref,
    chosen_ref,
    potential_ref,
    field_ref,
    near_wide,
    leaf_wide,
    mid_wide,
    uppers,
    leaf_flat,
    upper_rows_ref,
    spread,
    leaf_rows,
    mid_rows,
    operators,
    top_local,
    local_table,
    sums,
    sends,
    receives,
    upper_send,
    upper_receive,
):
    block_x, block_y, block_z = sizes
    columns = block_x * block_y
    width = block_z * SLOTS
    terms = down_ref.shape[1]
    offsets = plan_ref.shape[0] // 16
    padded_terms = operators.shape[1]

    at = tuple(lax.axis_index(axis) for axis in ("gx", "gy", "gz"))
    devices = numbers[0] * numbers[1] * numbers[2]
    rank = (at[0] * numbers[1] + at[1]) * numbers[2] + at[2]

    def coordinates(step):
        other = lax.rem(rank + step, devices)
        return (
            other // (numbers[1] * numbers[2]),
            lax.rem(other // numbers[2], numbers[1]),
            lax.rem(other, numbers[2]),
        )

    barrier = pltpu.get_barrier_semaphore()

    def greet(step, carry):
        pl.semaphore_signal(
            barrier, inc=1, device_id=coordinates(step), device_id_type=pl.DeviceIdType.MESH
        )
        return carry

    lax.fori_loop(1, devices, greet, 0)
    near_wide[1, 1 : 1 + block_x, 1 : 1 + block_y] = own_ref[...]
    own_slot = uppers.at[pl.ds(pl.multiple_of(rank * 8, 8), 8)]
    local_moments(
        sizes, data_ref, shift_ref, order_ref, local_table, leaf_flat, leaf_wide, mid_wide, own_slot
    )
    halves = (block_x // 2, block_y // 2)
    near_copies = halo_copies(near_wide, sizes, 1, numbers, at, sends.at[0], receives.at[0])
    leaf_copies = halo_copies(leaf_wide, sizes, 2, numbers, at, sends.at[1], receives.at[1])
    mid_copies = halo_copies(mid_wide, halves, 2, numbers, at, sends.at[2], receives.at[2])

    def upper_copy(step):
        return pltpu.make_async_remote_copy(
            src_ref=own_slot,
            dst_ref=own_slot,
            send_sem=upper_send.at[step],
            recv_sem=upper_receive.at[step],
            device_id=coordinates(step),
            device_id_type=pl.DeviceIdType.MESH,
        )

    def send_upper(step, carry):
        upper_copy(step).start()
        return carry

    def wait_upper(step, carry):
        upper_copy(step).wait()
        return carry

    pl.semaphore_wait(barrier, devices - 1)
    for copy in near_copies + leaf_copies + mid_copies:
        copy.start()
    lax.fori_loop(1, devices, send_upper, 0)

    def place(row, carry):
        start = row * terms
        base = jnp.minimum(start & -LANES, far_ref.shape[1] - 2 * LANES)
        base = pl.multiple_of(base, LANES)
        held = far_ref[:, pl.ds(base, 2 * LANES)].astype(F32)
        held = jnp.concatenate(
            [held, jnp.zeros((padded_terms - terms, 2 * LANES), F32)], axis=0
        )
        turned = pltpu.roll(held, (2 * LANES - (start - base)) & (2 * LANES - 1), 1)
        return turned[:, :LANES].astype(BF16)

    def place_pair(pair, carry):
        for which in range(2):
            operators[2 * pair + which, :, :LANES] = place(4 * pair + 2 * which, carry)
            operators[2 * pair + which, :, LANES:] = place(4 * pair + 2 * which + 1, carry)
        return carry

    lax.fori_loop(0, offsets // 4, place_pair, 0)

    lane = lax.broadcasted_iota(jnp.int32, (columns, width), 1)
    group = lane - lane % SLOTS
    turns = [group + (lane + step) % SLOTS for step in range(1, 9)]
    target_x = data_ref[0]
    target_y = data_ref[1]
    target_z = data_ref[2]
    for copy in near_copies:
        copy.wait()

    def fill(x, carry):
        for y in range(block_y + 2):
            low, own, high = (near_wide[0, x, y], near_wide[1, x, y], near_wide[2, x, y])
            moved = (
                jnp.concatenate([low[:, width - SLOTS :], own[:, : width - SLOTS]], axis=1),
                own,
                jnp.concatenate([own[:, SLOTS:], high[:, :SLOTS]], axis=1),
            )
            for move_y in range(3):
                if not 0 <= y - move_y < block_y:
                    continue
                for move_z in range(3):
                    for component in range(4):
                        spread[
                            (component * 3 + move_z) * 3 + move_y,
                            pl.ds(x * block_y + y - move_y, 1),
                            :,
                        ] = moved[move_z][component : component + 1]
        return carry

    lax.fori_loop(0, block_x + 2, fill, 0)

    def neighbour(which, totals):
        move_x = which // 9
        move_yz = which % 9
        move_y = move_yz // 3
        move_z = move_yz % 3
        slab = move_z * 3 + move_y
        rows = pl.ds(move_x * block_y, columns)
        shift_x = (move_x - 1).astype(F32)
        shift_y = (move_y - 1).astype(F32)
        shift_z = (move_z - 1).astype(F32)
        source = (
            spread[slab, rows, :] + shift_x,
            spread[9 + slab, rows, :] + shift_y,
            spread[18 + slab, rows, :] + shift_z,
            spread[27 + slab, rows, :],
        )
        own = which == 13

        def step(at, carry):
            held, totals = carry
            keep = jnp.where(own & (at == 0), 0.0, 1.0)
            sum_p, sum_x, sum_y, sum_z = totals
            for turn in range(8):
                if turn == 0:
                    s_x, s_y, s_z, s_q = held
                    s_q = s_q * keep
                else:
                    s_x, s_y, s_z, s_q = [
                        jnp.take_along_axis(value, turns[turn - 1], axis=1) for value in held
                    ]
                d_x = target_x - s_x
                d_y = target_y - s_y
                d_z = target_z - s_z
                inverse = lax.rsqrt(d_x * d_x + d_y * d_y + d_z * d_z + SOFTENING)
                weight = s_q * inverse
                sum_p = sum_p + weight
                cubic = weight * (inverse * inverse)
                sum_x = sum_x + cubic * d_x
                sum_y = sum_y + cubic * d_y
                sum_z = sum_z + cubic * d_z
            held = tuple(jnp.take_along_axis(value, turns[7], axis=1) for value in held)
            return held, (sum_p, sum_x, sum_y, sum_z)

        return lax.fori_loop(0, SLOTS // 8, step, (source, totals))[1]

    zero = jnp.zeros((columns, width), F32)
    near = lax.fori_loop(0, 27, neighbour, (zero, zero, zero, zero))

    row_of = lax.broadcasted_iota(jnp.int32, (8, LANES), 0)

    def sheets(held, cells, move):
        turned = pltpu.roll(held, (8 - (move + 2)) % 8, 0)
        if move == 3:
            turned = jnp.where(row_of % 2 == 0, turned, 0.0)
        if move == -3:
            turned = jnp.where(row_of % 2 == 1, turned, 0.0)
        upper = turned.astype(BF16).astype(F32)
        lower = pltpu.roll(turned - upper, cells, 0)
        made = jnp.where(row_of < cells, upper, lower)
        return jnp.where(row_of < 2 * cells, made, 0.0)

    for copy in leaf_copies + mid_copies:
        copy.wait()
    lax.fori_loop(1, devices, wait_upper, 0)
    wide_x, wide_y = leaf_wide.shape[1], leaf_wide.shape[2]
    leaf_rows[...] = jnp.zeros(leaf_rows.shape, F32)
    mid_rows[...] = jnp.zeros(mid_rows.shape, F32)

    def leaf_sheet(at, carry):
        x = at // wide_y
        y = at % wide_y
        held = jnp.concatenate(
            [leaf_wide[0, x, y][block_z - 2 :], leaf_wide[1, x, y], leaf_wide[2, x, y][:2]], axis=0
        )
        for move in range(-3, 4):
            leaf_rows[move + 3, x, y] = sheets(held, block_z, move)
        return carry

    lax.fori_loop(0, wide_x * wide_y, leaf_sheet, 0)
    mid_x, mid_y = mid_wide.shape[1], mid_wide.shape[2]

    def mid_sheet(at, carry):
        x = at // mid_y
        y = at % mid_y
        held = jnp.concatenate(
            [mid_wide[0, x, y], mid_wide[1, x, y], mid_wide[2, x, y], jnp.zeros((2, LANES), F32)],
            axis=0,
        )
        for move in range(-3, 4):
            mid_rows[move + 3, x, y] = sheets(held, block_z // 2, move)
        return carry

    lax.fori_loop(0, mid_x * mid_y, mid_sheet, 0)

    half_x, half_y = block_x // 2, block_y // 2
    upper_rows = chosen_ref.shape[1]
    all_upper = uppers[pl.ds(0, devices, stride=8), :]
    sorted_upper = exact(merge_ref[...], all_upper, (((1,), (0,)), ((), ())))
    tops = devices // 8
    merged = jnp.zeros((tops, terms), F32)
    for octant in range(8):
        merged = merged + apply(sorted_upper[octant * tops : (octant + 1) * tops, :terms], shift_ref[octant])
    root = jnp.sum(merged, axis=0, keepdims=True)
    merged = jnp.concatenate([merged, jnp.zeros((tops, LANES - terms), F32)], axis=1)
    both = jnp.concatenate(split_rows(jnp.concatenate([all_upper, merged], axis=0)), axis=1)

    def pick(group, carry):
        found = jnp.dot(
            chosen_ref[pl.ds(group * 4, 4)].reshape(4 * upper_rows, -1).astype(BF16),
            both,
            preferred_element_type=F32,
        )
        upper_rows_ref[pl.ds(group * 4, 4)] = found.reshape(4, upper_rows, 2 * LANES)
        return carry

    lax.fori_loop(0, offsets // 4, pick, 0)

    def gathered(row):
        at = row * 16
        move_z = plan_ref[at + 2]
        pieces = []
        for x in range(block_x):
            for y in range(block_y):
                pieces.append(leaf_rows[move_z, plan_ref[at + 4 + x % 2] + x, plan_ref[at + 6 + y % 2] + y])
        for x in range(half_x):
            for y in range(half_y):
                pieces.append(mid_rows[move_z, plan_ref[at + 8 + x % 2] + x, plan_ref[at + 10 + y % 2] + y])
        pieces.append(upper_rows_ref[row, :, :LANES])
        pieces.append(upper_rows_ref[row, :, LANES:])
        return jnp.concatenate(pieces, axis=0).astype(BF16)

    def far_step(pair, total):
        added = []
        for which in range(2):
            row = 4 * pair + 2 * which
            left = jnp.concatenate([gathered(row), gathered(row + 1)], axis=1)
            added.append(
                lax.dot_general(left, operators[2 * pair + which], NT, preferred_element_type=F32)
            )
        return total + (added[0] + added[1])

    leaf_count = columns * 8
    mid_count = half_x * half_y * 8
    total_rows = leaf_count + mid_count + 2 * upper_rows
    sums[...] = lax.fori_loop(
        0, offsets // 4, far_step, jnp.zeros((total_rows, padded_terms), F32)
    )
    first = leaf_count + mid_count
    far_high = sums[first : first + upper_rows, :terms] + sums[first + upper_rows :, :terms]
    lattice = apply(jnp.broadcast_to(root, (8, terms)), lattice_ref[...])
    top_local[...] = 0.125 * (far_high + lattice[:1])
    parent = top_local[pl.ds(where_ref[0] + 1, 1), :]
    upper = 0.25 * far_high[:1] + apply(jnp.broadcast_to(parent, (8, terms)), down_ref[where_ref[1]])[:1]
    upper = jnp.broadcast_to(upper, (8, terms))
    half_z = block_z // 2
    mids = jnp.concatenate([apply(upper, down_ref[octant])[:1] for octant in range(8)], axis=0)
    far_mids = []
    for column in range(half_x * half_y):
        held = sums[leaf_count + column * 8 : leaf_count + column * 8 + 8, :terms]
        far_mids.append(held[:half_z] + held[half_z : 2 * half_z])
    mids = mids + 0.5 * jnp.concatenate(far_mids, axis=0)
    pieces = [apply(mids, down_ref[octant]) for octant in range(8)]
    downs = exact(order_ref[...], jnp.concatenate(pieces, axis=0), TN)
    picker = cell_picker(block_z, block_z)
    for column in range(columns):
        held = sums[column * 8 : column * 8 + 8, :terms]
        local = held[:block_z] + held[block_z : 2 * block_z]
        local = local + downs[column * block_z : (column + 1) * block_z]
        local_table[pl.ds(column, terms, stride=columns), :] = exact(local, picker, TN)

    made = monomial_map(powers_of(target_x - 0.5), powers_of(target_y - 0.5), target_z - 0.5)
    out_p, out_x, out_y, out_z = near
    for row, key in enumerate(exponent_table(ORDER)):
        power_x, power_y, power_z = [int(v) for v in key]
        local = local_table[row * columns : (row + 1) * columns, :]
        out_p = out_p + local * made[(power_x, power_y, power_z)]
        if power_x:
            out_x = out_x - (float(power_x) * local) * made[(power_x - 1, power_y, power_z)]
        if power_y:
            out_y = out_y - (float(power_y) * local) * made[(power_x, power_y - 1, power_z)]
        if power_z:
            out_z = out_z - local * made[(power_x, power_y, 0)]
    live = live_ref[...]
    potential_ref[...] = out_p * live
    field_ref[0] = out_x * live
    field_ref[1] = out_y * live
    field_ref[2] = out_z * live


def plan_table(block_x, block_y):
    shifts = offset_table()
    plan = np.zeros((shifts.shape[0], 16), np.int32)
    for row, shift in enumerate(shifts):
        for axis in range(3):
            plan[row, axis] = shift[axis] + 3
        for axis in range(2):
            block = (block_x, block_y)[axis]
            for odd in range(2):
                admitted = -2 - odd <= shift[axis] <= 3 - odd
                plan[row, 4 + 2 * axis + odd] = shift[axis] + 2 if admitted else block + 4
                plan[row, 8 + 2 * axis + odd] = shift[axis] + 2 if admitted else block // 2 + 4
    return plan.reshape(-1)


def per_device(
    positions, charges, counts, moment_shift, far_operators, local_shift, lattice_operator
):
    block_x, block_y, column = charges.shape
    block_z = column // SLOTS
    sizes = (block_x, block_y, block_z)
    number_x = lax.axis_size("gx")
    number_y = lax.axis_size("gy")
    number_z = lax.axis_size("gz")
    index_x = lax.axis_index("gx")
    index_y = lax.axis_index("gy")
    index_z = lax.axis_index("gz")
    terms = moment_shift.shape[1]
    padded_terms = (terms + 15) // 16 * 16
    columns = block_x * block_y
    leaves = columns * block_z
    slot_of = jnp.arange(column, dtype=jnp.int32) % SLOTS
    live_mask = (slot_of[None, None, :] < jnp.repeat(counts, SLOTS, axis=2)).astype(F32)
    weights = charges * live_mask
    stacked = jnp.concatenate([positions, weights[None]], axis=0)
    order = jnp.asarray(permutation(*sizes))
    vmem = pl.BlockSpec(memory_space=pltpu.VMEM)
    smem = pl.BlockSpec(memory_space=pltpu.SMEM)
    top_count = number_x * number_y * number_z // 8
    top_sizes = (number_x // 2, number_y // 2, number_z // 2)
    shifts = offset_table()
    offsets = shifts.shape[0]
    upper_rows = (1 + top_count + 7) // 8 * 8
    at = (index_x, index_y, index_z)
    numbers = (number_x, number_y, number_z)
    picked = 0
    admitted = True
    for axis in range(3):
        picked = picked * numbers[axis] + (at[axis] + shifts[:, axis]) % numbers[axis]
        odd = at[axis] % 2
        admitted = admitted & (shifts[:, axis] >= -2 - odd) & (shifts[:, axis] <= 3 - odd)
    picked = jnp.where(admitted, picked, -1)
    entries = number_x * number_y * number_z
    static = np.full((offsets, upper_rows), -1, np.int32)
    for row in range(offsets):
        for box in range(top_count):
            spot = (
                box // (top_sizes[1] * top_sizes[2]),
                box // top_sizes[2] % top_sizes[1],
                box % top_sizes[2],
            )
            moved = [(spot[axis] + int(shifts[row, axis])) % top_sizes[axis] for axis in range(3)]
            static[row, 1 + box] = (
                entries + (moved[0] * top_sizes[1] + moved[1]) * top_sizes[2] + moved[2]
            )
    index = jnp.where(jnp.arange(upper_rows)[None, :] == 0, picked[:, None], jnp.asarray(static))
    chosen = (index[:, :, None] == jnp.arange(entries + top_count)[None, None, :]).astype(F32)
    parent = (index_x // 2 * top_sizes[1] + index_y // 2) * top_sizes[2] + index_z // 2
    octant = index_x % 2 * 4 + index_y % 2 * 2 + index_z % 2
    where = jnp.stack([parent, octant]).astype(jnp.int32)
    wide_x, wide_y = block_x + 5, block_y + 5
    half_x, half_y = block_x // 2, block_y // 2
    potential, field_out = pl.pallas_call(
        lambda *refs: field_kernel(sizes, numbers, *refs),
        out_shape=(
            jax.ShapeDtypeStruct((columns, column), F32),
            jax.ShapeDtypeStruct((3, columns, column), F32),
        ),
        in_specs=[smem, smem] + [vmem] * 10,
        out_specs=(vmem, vmem),
        scratch_shapes=[
            pltpu.VMEM((3, block_x + 2, block_y + 2, 4, column), F32),
            pltpu.VMEM((3, block_x + 4, block_y + 4, block_z, LANES), F32),
            pltpu.VMEM((3, half_x + 4, half_y + 4, block_z // 2, LANES), F32),
            pltpu.VMEM((entries * 8 + 8, LANES), F32),
            pltpu.VMEM((leaves, LANES), F32),
            pltpu.VMEM((offsets, upper_rows, 2 * LANES), F32),
            pltpu.VMEM((36, (block_x + 4) * block_y, column), F32),
            pltpu.VMEM((7, block_x + 4 + block_x, block_y + 4 + block_y, 8, LANES), F32),
            pltpu.VMEM((7, half_x + 4 + half_x, half_y + 4 + half_y, 8, LANES), F32),
            pltpu.VMEM((offsets // 2, padded_terms, 2 * LANES), BF16),
            pltpu.VMEM((upper_rows, terms), F32),
            pltpu.VMEM(((padded_terms + 1) * columns, column), F32),
            pltpu.VMEM((columns * 8 + half_x * half_y * 8 + 2 * upper_rows, padded_terms), F32),
            pltpu.SemaphoreType.DMA((3, 27)),
            pltpu.SemaphoreType.DMA((3, 27)),
            pltpu.SemaphoreType.DMA((entries,)),
            pltpu.SemaphoreType.DMA((entries,)),
        ],
        compiler_params=pltpu.CompilerParams(
            vmem_limit_bytes=60 * 1024 * 1024, collective_id=0, has_side_effects=True
        ),
        name="fields",
    )(
        jnp.asarray(plan_table(block_x, block_y)),
        where,
        jnp.transpose(stacked, (1, 2, 0, 3)),
        stacked.reshape(4, columns, column),
        live_mask.reshape(columns, column),
        moment_shift,
        far_operators,
        local_shift,
        lattice_operator,
        order,
        jnp.asarray(permutation(*numbers)),
        chosen,
    )
    return (
        potential.reshape(block_x, block_y, column),
        field_out.reshape(3, block_x, block_y, column),
    )


def solution(mesh):
    placed = (
        P(None, "gx", "gy", "gz"),
        P("gx", "gy", "gz"),
        P("gx", "gy", "gz"),
        P(),
        P(),
        P(),
        P(),
    )
    return jax.shard_map(
        per_device,
        mesh=mesh,
        in_specs=placed,
        out_specs=(P("gx", "gy", "gz"), P(None, "gx", "gy", "gz")),
        check_vma=False,
    )
```

profile of v0, /device:TPU:0, one launch (start us, length us, event | category | flops | bytes accessed | tf_op | source)
XLA Modules:
  0.0 86.1 jit_solution(4853445425425897028)
XLA Ops:
  0.6 0.0 copy-start.3
  0.6 0.0 copy-start.4
  0.7 0.0 copy-start.2
  0.7 0.0 copy-start
  0.7 0.0 copy-start.1
  0.7 0.8 fusion.5
  1.5 1.0 %broadcast_select_fusion = s32[316,8]{1,0:T(8,128)S(1)} fusion(s32[316,8]{1,0:T(8,128)} %constant.130.clone, s32[316]{0:T(512)S(1)} %fusion.5, pred[8]{0:T(512)(128)(4,1)S(1)} %iota_compare_fusion.1), kind=kLoop, calls=%fused_computation.2 | loop fusion | flops 2528 | bytes 21496 | tf_op jit(solution)/shard_map/jit(_where)/select_n | solution.py:586
  2.6 1.7 %fusion.refs_11_ = f32[316,8,36]{2,1,0:T(8,128)} fusion(s32[316,8]{1,0:T(8,128)S(1)} %broadcast_select_fusion), kind=kLoop, calls=%fused_computation.1 | loop fusion | flops 182016 | bytes 374144 | tf_op jit(solution)/shard_map/convert_element_type | solution.py:587
  4.2 0.7 pad_add_fusion.refs_1_
  4.9 0.0 copy-done.3
  4.9 0.1 broadcast_in_dim.31
  5.0 0.1 reshape.37
  5.1 0.0 copy-done.4
  5.1 0.0 copy-done.2
  5.1 0.6 maximum_bitcast_fusion.refs_2_
  5.8 0.6 pad_maximum_fusion.refs_3_
  6.4 0.1 reshape.38
  6.5 0.6 compare_convert_fusion.refs_4_
  7.1 0.0 copy-done
  7.1 0.7 copy.23.refs_5_
  7.8 0.0 copy-done.1
  7.8 0.7 copy.24.refs_7_
  8.5 75.0 %fields.1 = (f32[16,128]{1,0:T(8,128)}, f32[3,16,128]{2,1,0:T(8,128)}) custom-call(s32[5056]{0:T(1024)} %constant.131.clone.refs_0_, s32[2]{0:T(128)} %pad_add_fusion.refs_1_, f32[4,4,4,128]{3,2,1,0:T(4,128)} %maximum_bitcast_fusion.refs_2_, f32[4,16,128]{2,1,0:T(8,128)} %pad_maximum_fusion.refs_3_, f32[16,128]{1,0:T(8,128)} %compare_convert_fusion.refs_4_, ...), custom_call_target="tpu_custom_call" | custom-call | tf_op jit(solution)/shard_map/fields/pallas_call | solution.py:593
  83.5 1.3 %copy.27 = f32[4,4,128]{2,1,0:T(4,128)} copy(f32[4,4,128]{2,1,0:T(4,128)} %bitcast.13) | data formatting | bytes 16384
  84.8 1.3 %copy.28 = f32[3,4,4,128]{3,2,1,0:T(4,128)} copy(f32[3,4,4,128]{3,2,1,0:T(4,128)} %bitcast.12) | data formatting | bytes 49152
  (4 shorter events, 0.0 us)
Async XLA Ops:
  0.6 4.3 %copy-start.3 = (s32[4,4,4]{2,1,0:T(4,128)S(1)}, s32[4,4,4]{2,1,0:T(4,128)}, u32[]{:S(2)}) copy-start(s32[4,4,4]{2,1,0:T(4,128)} %param.22) | copy-start | bytes 772
  0.6 4.4 %copy-start.4 = (f32[4,4,128]{2,1,0:T(4,128)S(1)}, f32[4,4,128]{2,1,0:T(4,128)}, u32[]{:S(2)}) copy-start(f32[4,4,128]{2,1,0:T(4,128)} %param.21) | copy-start | bytes 24580
  0.7 4.4 %copy-start.2 = (f32[3,4,4,128]{3,2,1,0:T(4,128)S(1)}, f32[3,4,4,128]{3,2,1,0:T(4,128)}, u32[]{:S(2)}) copy-start(f32[3,4,4,128]{3,2,1,0:T(4,128)} %param.20) | copy-start | bytes 73732
  0.7 6.4 %copy-start = (bf16[8,81,81]{2,0,1:T(8,128)(2,1)S(1)}, bf16[8,81,81]{2,0,1:T(8,128)(2,1)}, u32[]{:S(2)}) copy-start(bf16[8,81,81]{2,0,1:T(8,128)(2,1)} %param.23) | copy-start | bytes 314932
  0.7 7.1 %copy-start.1 = (bf16[8,81,81]{2,0,1:T(8,128)(2,1)S(1)}, bf16[8,81,81]{2,0,1:T(8,128)(2,1)}, u32[]{:S(2)}) copy-start(bf16[8,81,81]{2,0,1:T(8,128)(2,1)} %param.25) | copy-start | bytes 314932
where the time goes:
time: 86.3 us; the launch traced here: 86.1 us
  Pallas kernels  75 us (87%)
  other arithmetic  6.03 us (7%)
  local copies, waits for them, and re-layouts  4.33 us (5%)
    pallas_call x1, Pallas kernels, per_device(): pl.pallas_call(lambda *refs: field_kernel(sizes, numbers, *refs), out_sha...  75 us
    unnamed x15, local copies, waits for them, and re-layouts  4.08 us

commit v1 on v0

v1 whole, which is shorter than its diff:
```python
import jax
import jax.numpy as jnp
import numpy as np
from jax import lax
from jax.experimental import pallas as pl
from jax.experimental.pallas import tpu as pltpu
from jax.sharding import PartitionSpec as P

ORDER = 8
SLOTS = 32
SOFTENING = 0.0625
LANES = 128
HALO = 2
F32 = jnp.float32
BF16 = jnp.bfloat16
NT = (((1,), (1,)), ((), ()))
NN = (((1,), (0,)), ((), ()))
PLAN = 16
GROUP = 4
STEPS = 28


def offset_table():
    listed = []
    for shift_x in range(-3, 4):
        for shift_y in range(-3, 4):
            for shift_z in range(-3, 4):
                if max(abs(shift_x), abs(shift_y), abs(shift_z)) >= 2:
                    listed.append((shift_x, shift_y, shift_z))
    return np.array(listed, dtype=np.int32)


def exponent_table(degree):
    listed = []
    for accumulated in range(degree + 1):
        for height in (0, 1):
            for power_x in range(accumulated - height + 1):
                listed.append((power_x, accumulated - height - power_x, height))
    return np.array(listed, dtype=np.int32)


ROW_OF = {tuple(int(v) for v in key): row for row, key in enumerate(exponent_table(ORDER))}


def split_rows(data):
    upper = data.astype(BF16)
    lower = (data - upper.astype(F32)).astype(BF16)
    return upper, lower


def apply(data, operator):
    upper, lower = split_rows(data)
    rows = data.shape[0]
    both = jnp.concatenate([upper.astype(F32), lower.astype(F32)], axis=0).astype(BF16)
    found = lax.dot_general(both, operator, NT, preferred_element_type=F32)
    return found[:rows] + found[rows:]


def powers_of(values):
    listed = [jnp.ones_like(values)]
    for exponent in range(ORDER):
        listed.append(listed[-1] * values)
    return listed


def admits(shift, odd):
    return -2 - odd <= shift <= 3 - odd


def leaf_start(shift):
    return {-3: 7, 3: 8}.get(shift, shift + 2)


def plan_table(block_x, block_z):
    shifts = offset_table()
    wide_x, wide_z = block_x + 2 * HALO, block_z + 2 * HALO
    starts = 2 * (wide_x - 1) // 2 + 4
    triples = STEPS * GROUP
    assert 3 * triples >= shifts.shape[0]
    plan = np.zeros((triples * 3, PLAN), np.int32)
    none_leaf = 7 * wide_z * starts
    mid_x, mid_z = block_x // 2 + 4, block_z // 2 + 4
    none_mid = 7 * mid_z * mid_x
    plan[:, :4] = none_leaf
    plan[:, 4:8] = none_mid
    plan[:, 8:11] = 7
    for row, (dx, dy, dz) in enumerate(shifts):
        for z in range(block_z):
            if admits(dz, z % 2):
                plan[row, z] = ((dy + 3) * wide_z + z + 2 + dz) * starts + leaf_start(dx)
        for x in range(2):
            for z in range(2):
                if admits(dz, z) and admits(dx, x):
                    plan[row, 4 + x * 2 + z] = ((dy + 3) * mid_z + z + 2 + dz) * mid_x + x + 2 + dx
        plan[row, 8:11] = (dx + 3, dy + 3, dz + 3)
    return plan.reshape(-1), triples, none_leaf, none_mid, starts


def field_kernel(
    sizes,
    numbers,
    layout,
    plan_ref,
    positions_hbm,
    charges_hbm,
    counts_hbm,
    shift_hbm,
    far_hbm,
    down_hbm,
    lattice_hbm,
    potential_ref,
    field_ref,
    positions,
    charges,
    counts,
    shift_raw,
    far,
    down_raw,
    lattice,
    raw,
    wide,
    targets,
    partial,
    moments_high,
    moments_low,
    mids,
    shift_rows,
    down_rows,
    uppers,
    operators,
    sources,
    leaf_pages,
    mid_high,
    mid_low,
    mid_pages,
    upper_pages,
    top_pages,
    sums,
    local_rows,
    table,
    loads,
    sends,
    receives,
    mid_send,
    mid_receive,
):
    block_x, block_y, block_z = sizes
    triples, none_leaf, none_mid, starts = layout
    wide_x, wide_z = block_x + 2 * HALO, block_z + 2 * HALO
    rows_y = block_y + 2 * HALO
    columns = block_x * block_y
    leaves = columns * block_z
    terms = lattice.shape[0]
    padded_terms = operators.shape[1]
    offsets = offset_table().shape[0]
    at = tuple(lax.axis_index(axis) for axis in ("gx", "gy", "gz"))
    devices = numbers[0] * numbers[1] * numbers[2]
    rank = (at[0] * numbers[1] + at[1]) * numbers[2] + at[2]
    barrier = pltpu.get_barrier_semaphore()

    def coordinates(step):
        other = lax.rem(rank + step, devices)
        return (
            lax.div(other, numbers[1] * numbers[2]),
            lax.rem(lax.div(other, numbers[2]), numbers[1]),
            lax.rem(other, numbers[2]),
        )

    staged = [
        pltpu.make_async_copy(positions_hbm, positions, loads.at[0]),
        pltpu.make_async_copy(charges_hbm, charges, loads.at[1]),
        pltpu.make_async_copy(counts_hbm, counts, loads.at[2]),
        pltpu.make_async_copy(shift_hbm, shift_raw, loads.at[3]),
        pltpu.make_async_copy(far_hbm, far.at[:, pl.ds(0, far_hbm.shape[1])], loads.at[4]),
        pltpu.make_async_copy(down_hbm, down_raw, loads.at[5]),
        pltpu.make_async_copy(lattice_hbm, lattice, loads.at[6]),
    ]
    for copy in staged:
        copy.start()

    def greet(step, carry):
        pl.semaphore_signal(
            barrier, inc=1, device_id=coordinates(step), device_id_type=pl.DeviceIdType.MESH
        )
        return carry

    lax.fori_loop(1, devices, greet, 0)

    lane = lax.broadcasted_iota(jnp.int32, (columns, LANES), 1)
    group = lane // SLOTS
    row8 = lax.broadcasted_iota(jnp.int32, (8, LANES), 0)
    for copy in staged[:3]:
        copy.wait()
    held = jnp.concatenate([counts[x] for x in range(block_x)], axis=0)
    limit = jnp.broadcast_to(held[:, 0:1], (columns, LANES))
    for z in range(1, block_z):
        limit = jnp.where(group == z, jnp.broadcast_to(held[:, z : z + 1], (columns, LANES)), limit)
    live = (lane % SLOTS < limit).astype(F32)
    parts = [
        jnp.concatenate([positions[c, x] for x in range(block_x)], axis=0) for c in range(3)
    ]
    parts.append(jnp.concatenate([charges[x] for x in range(block_x)], axis=0) * live)
    pieces = []
    for z in range(block_z):
        made = None
        for c in range(4):
            turn = (c - z) * SLOTS % LANES
            moved = pltpu.roll(parts[c], turn, 1) if turn else parts[c]
            made = moved if made is None else jnp.where(group == c, moved, made)
        pieces.append(made)
        for x in range(block_x):
            for pair in range(block_y // 2):
                start = x * block_y + 2 * pair
                raw[1 + pair, HALO + z, HALO + x] = made[start : start + 2]
    own = jnp.concatenate(pieces + pieces, axis=0)
    targets[...] = own.T

    pl.semaphore_wait(barrier, devices - 1)
    copies = []
    pairs = block_y // 2

    def span(move, size, halo):
        if move == 1:
            return pl.ds(size, halo), pl.ds(0, halo)
        if move == -1:
            return pl.ds(halo, halo), pl.ds(size + halo, halo)
        return pl.ds(halo, size), pl.ds(halo, size)

    for count in range(27):
        moves = (count // 9 - 1, count // 3 % 3 - 1, count % 3 - 1)
        if moves == (0, 0, 0):
            continue
        target = tuple(
            lax.rem(at[axis] + moves[axis] + numbers[axis], numbers[axis]) for axis in range(3)
        )
        from_x, to_x = span(moves[0], block_x, HALO)
        from_y, to_y = span(moves[1], pairs, 1)
        from_z, to_z = span(moves[2], block_z, HALO)
        copies.append(
            pltpu.make_async_remote_copy(
                src_ref=raw.at[from_y, from_z, from_x],
                dst_ref=raw.at[to_y, to_z, to_x],
                send_sem=sends.at[count],
                recv_sem=receives.at[count],
                device_id=target,
                device_id_type=pl.DeviceIdType.MESH,
            )
        )
    for copy in copies:
        copy.start()

    partial[pl.ds(terms * 8, partial.shape[0] - terms * 8), :] = jnp.zeros(
        (partial.shape[0] - terms * 8, LANES), F32
    )

    def moments(at_x, at_y, at_z, charge):
        quarter = SLOTS // 8
        centred_z = at_z - 0.5
        centred_y = at_y - 0.5
        powers_x = [value * charge for value in powers_of(at_x - 0.5)]
        power_y = None
        for b in range(ORDER + 1):
            power_y = None if b == 0 else (centred_y if b == 1 else power_y * centred_y)
            for a in range(ORDER + 1 - b):
                flat = powers_x[a] if b == 0 else powers_x[a] * power_y
                for height in (0, 1):
                    if a + b + height > ORDER:
                        continue
                    made = flat * centred_z if height else flat
                    total = made[:8]
                    for piece in range(1, quarter):
                        total = total + made[piece * 8 : piece * 8 + 8]
                    row = ROW_OF[(a, b, height)]
                    partial[row * 8 : row * 8 + 8, :] = total
        found = partial[pl.ds(0, padded_terms, stride=8), :]
        for line in range(1, 8):
            found = found + partial[pl.ds(line, padded_terms, stride=8), :]
        found = jnp.concatenate([found, jnp.zeros((LANES - padded_terms, LANES), F32)], axis=0)
        return found.T

    def rows_from(raw_ref, out_ref):
        out_ref[...] = jnp.zeros(out_ref.shape, F32)
        out_ref[:, :terms] = raw_ref[...].astype(F32).reshape(terms * 8, terms)

    def octant_of(ref, octant):
        return ref[pl.ds(octant, terms, stride=8), :].astype(BF16)

    own_moments = moments(
        targets[:SLOTS], targets[SLOTS : 2 * SLOTS], targets[2 * SLOTS : 3 * SLOTS], targets[3 * SLOTS :]
    )[:leaves]
    staged[3].wait()
    rows_from(shift_raw, shift_rows)
    leaf_row = lax.broadcasted_iota(jnp.int32, (leaves, terms), 0)
    leaf_octant = (
        4 * (leaf_row // block_y % 2) + 2 * (leaf_row % 2) + leaf_row // columns % 2
    )
    lifted = jnp.zeros((leaves, terms), F32)
    for octant in range(8):
        found = apply(own_moments, octant_of(shift_rows, octant))
        lifted = jnp.where(leaf_octant == octant, found, lifted)
    lines = []
    for z in range(block_z // 2):
        both = lifted[2 * z * columns : (2 * z + 1) * columns] + lifted[(2 * z + 1) * columns : (2 * z + 2) * columns]
        for x in range(block_x // 2):
            held = both[x * 8 : x * 8 + 8]
            held = held[:4] + held[4:]
            for y in range(block_y // 2):
                lines.append(held[2 * y : 2 * y + 1] + held[2 * y + 1 : 2 * y + 2])
    spare = jnp.zeros((8, LANES - terms), F32)
    own_slot = mids.at[pl.ds(pl.multiple_of(rank * 8, 8), 8)]
    own_slot[...] = jnp.concatenate([jnp.concatenate(lines, axis=0), spare], axis=1)

    def mid_copy(step):
        return pltpu.make_async_remote_copy(
            src_ref=own_slot,
            dst_ref=own_slot,
            send_sem=mid_send.at[step],
            recv_sem=mid_receive.at[step],
            device_id=coordinates(step),
            device_id_type=pl.DeviceIdType.MESH,
        )

    def send_mid(step, carry):
        mid_copy(step).start()
        return carry

    def wait_mid(step, carry):
        mid_copy(step).wait()
        return carry

    lax.fori_loop(1, devices, send_mid, 0)

    staged[4].wait()
    far[:, pl.ds(far_hbm.shape[1], 2 * LANES)] = jnp.zeros((terms, 2 * LANES), BF16)
    tall = lax.broadcasted_iota(jnp.int32, (padded_terms, LANES), 1)

    def place(triple, carry):
        start = triple * (3 * terms)
        turn = lax.rem(start, LANES)
        base = pl.multiple_of(start - turn, LANES)
        back = lax.rem(LANES - turn, LANES)
        turned = []
        for tile in range(3):
            held = far[:, pl.ds(pl.multiple_of(base + tile * LANES, LANES), LANES)].astype(F32)
            held = jnp.concatenate([held, jnp.zeros((padded_terms - terms, LANES), F32)], axis=0)
            turned.append(pltpu.roll(held, back, 1))
        kept = tall < LANES - turn
        for tile in range(2):
            found = jnp.where(kept, turned[tile], turned[tile + 1])
            operators[triple, :, tile * LANES : (tile + 1) * LANES] = found.astype(BF16)
        return carry

    used = operators.shape[0]
    lax.fori_loop(0, used, place, 0, unroll=2)

    strides = (numbers[1] * numbers[2], numbers[2], 1)
    top_sizes = tuple(number // 2 for number in numbers)
    top_strides = (top_sizes[1] * top_sizes[2], top_sizes[2], 1)
    tops = devices // 8
    for axis in range(3):
        odd = lax.rem(at[axis], 2)
        for entry in range(7):
            shift = entry - 3
            size = numbers[axis]
            place_at = lax.rem(at[axis] + shift + 4 * size, size) * strides[axis]
            if shift == -3:
                place_at = jnp.where(odd == 1, place_at, 4 * devices)
            if shift == 3:
                place_at = jnp.where(odd == 0, place_at, 4 * devices)
            table[axis * 8 + entry] = place_at
            size = top_sizes[axis]
            table[24 + axis * 8 + entry] = (
                lax.rem(lax.div(at[axis], 2) + shift + 4 * size, size) * top_strides[axis]
            )
        table[axis * 8 + 7] = jnp.int32(4 * devices)
        table[24 + axis * 8 + 7] = jnp.int32(4 * devices)

    for copy in copies:
        copy.wait()
    guard = 8
    for ref in (wide, moments_high, moments_low):
        ref[:guard, :] = jnp.zeros((guard, LANES), F32)
        ref[ref.shape[0] - guard :, :] = jnp.zeros((guard, LANES), F32)

    def widen(z, carry):
        for x in range(wide_x):
            column = jnp.concatenate([raw[pair, z, x] for pair in range(pairs + 2)], axis=0)
            wide[pl.ds(pl.multiple_of(guard + (z * wide_x + x) * rows_y, 8), rows_y), :] = column
        return carry

    lax.fori_loop(0, wide_z, widen, 0)

    def window(tile, carry):
        start = pl.multiple_of(guard + tile * LANES, 8)
        turned = wide[pl.ds(start, LANES), :].T
        found = moments(
            turned[:SLOTS], turned[SLOTS : 2 * SLOTS], turned[2 * SLOTS : 3 * SLOTS], turned[3 * SLOTS :]
        )
        upper = found.astype(BF16).astype(F32)
        moments_high[pl.ds(start, LANES), :] = upper
        moments_low[pl.ds(start, LANES), :] = (found - upper).astype(BF16).astype(F32)
        return carry

    lax.fori_loop(0, wide_x * wide_z * rows_y // LANES, window, 0)

    near_shifts = [(x, y, z) for x in (-1, 0, 1) for y in (-1, 0, 1) for z in (-1, 0, 1)]
    lane8 = lax.broadcasted_iota(jnp.int32, (8, LANES), 1)
    group8 = lane8 // SLOTS

    def shifted(shift):
        moved = jnp.where(
            group8 == 0,
            float(shift[0]),
            jnp.where(group8 == 1, float(shift[1]), jnp.where(group8 == 2, float(shift[2]), 0.0)),
        )
        found = []
        for z in range(block_z):
            for x in range(0, block_x, 2):
                spot = (z + HALO + shift[2]) * wide_x + x + HALO + shift[0]
                low = guard + spot * rows_y + HALO + shift[1]
                high = low + rows_y - block_y
                held = jnp.where(row8 < block_y, wide[low : low + 8, :], wide[high : high + 8, :])
                found.append(held + moved)
        return found

    for pair in range((len(near_shifts) + 1) // 2):
        first = shifted(near_shifts[2 * pair])
        if 2 * pair + 1 < len(near_shifts):
            second = shifted(near_shifts[2 * pair + 1])
        else:
            second = [jnp.where(group8 < 3, value, 0.0) for value in first]
        sources[pair * LANES : (pair + 1) * LANES, :] = jnp.concatenate(first + second, axis=0).T

    def third(value):
        return (value, pltpu.roll(value, terms, 1), pltpu.roll(value, 2 * terms - LANES, 1))

    odd_line = row8 % 2 == 1

    def fill_pages(z, carry):
        for shift in range(-3, 4):
            turned = []
            for x in range(wide_x):
                start = guard + (z * wide_x + x) * rows_y + HALO + shift
                page = jnp.where(
                    row8 < block_y,
                    moments_high[pl.ds(start, 8), :],
                    moments_low[pl.ds(start - block_y, 8), :],
                )
                if shift == -3:
                    page = jnp.where(odd_line, page, 0.0)
                if shift == 3:
                    page = jnp.where(odd_line, 0.0, page)
                turned.append(third(page))
            spot = ((shift + 3) * wide_z + z) * starts
            zero = jnp.zeros((8, LANES), F32)
            for kind in range(3):
                listed = [(x, turned[x][kind], turned[x + 1][kind]) for x in range(wide_x - 1)]
                listed.append((7, zero, turned[0][kind]))
                listed.append((9, zero, turned[2][kind]))
                listed.append((8, turned[5][kind], zero))
                listed.append((10, turned[7][kind], zero))
                for entry, low, high in listed:
                    leaf_pages[kind, spot + entry] = jnp.concatenate([low, high], axis=0).astype(BF16)
        return carry

    lax.fori_loop(0, wide_z, fill_pages, 0)
    for kind in range(3):
        for entry in range(3):
            leaf_pages[kind, none_leaf + entry] = jnp.zeros((16, LANES), BF16)

    lax.fori_loop(1, devices, wait_mid, 0)
    mid_x, mid_z = block_x // 2 + 4, block_z // 2 + 4
    for ref in (mid_high, mid_low):
        ref[:guard, :] = jnp.zeros((guard, LANES), F32)
        ref[ref.shape[0] - guard :, :] = jnp.zeros((guard, LANES), F32)
    around = []
    for count in range(27):
        moves = (count // 9 - 1, count // 3 % 3 - 1, count % 3 - 1)
        there = [lax.rem(at[axis] + moves[axis] + numbers[axis], numbers[axis]) for axis in range(3)]
        around.append(((there[0] * numbers[1] + there[1]) * numbers[2] + there[2]) * 8)
    for z in range(mid_z):
        for x in range(mid_x):
            line = (z % 2 * 2 + x % 2) * 2
            listed = []
            for y in range(3):
                base = around[(x // 2 * 3 + y) * 3 + z // 2]
                listed.append(mids[pl.ds(base + line, 2), :])
            listed.append(jnp.zeros((2, LANES), F32))
            held = jnp.concatenate(listed, axis=0)
            upper = held.astype(BF16).astype(F32)
            start = guard + (z * mid_x + x) * 8
            mid_high[start : start + 8, :] = upper
            mid_low[start : start + 8, :] = (held - upper).astype(BF16).astype(F32)

    def fill_mids(z, carry):
        for x in range(mid_x):
            for shift in range(-3, 4):
                start = guard + (z * mid_x + x) * 8 + 2 + shift
                page = jnp.where(
                    row8 < 4,
                    jnp.where(row8 < 2, mid_high[pl.ds(start, 8), :], mid_low[pl.ds(start - 2, 8), :]),
                    jnp.where(row8 < 6, mid_high[pl.ds(start - 4, 8), :], mid_low[pl.ds(start - 6, 8), :]),
                )
                if shift == -3:
                    page = jnp.where(odd_line, page, 0.0)
                if shift == 3:
                    page = jnp.where(odd_line, 0.0, page)
                for kind, value in enumerate(third(page)):
                    mid_pages[kind, ((shift + 3) * mid_z + z) * mid_x + x] = value
        return carry

    lax.fori_loop(0, mid_z, fill_mids, 0)
    for kind in range(3):
        mid_pages[kind, none_mid] = jnp.zeros((8, LANES), F32)

    raised = jnp.zeros((devices, terms), F32)
    for octant in range(8):
        line = (octant % 2 * 2 + octant // 4) * 2 + octant // 2 % 2
        raised = raised + apply(mids[pl.ds(line, devices, stride=8), :], octant_of(shift_rows, octant))
    raised = jnp.concatenate([raised, jnp.zeros((devices, LANES - terms), F32)], axis=1)
    uppers[:devices, :] = raised
    rank_row = lax.broadcasted_iota(jnp.int32, (devices, terms), 0)
    rank_octant = (
        4 * (rank_row // strides[0] % 2) + 2 * (rank_row // strides[1] % 2) + rank_row % 2
    )
    lifted = jnp.zeros((devices, terms), F32)
    for octant in range(8):
        found = apply(raised, octant_of(shift_rows, octant))
        lifted = jnp.where(rank_octant == octant, found, lifted)
    root = jnp.sum(lifted, axis=0, keepdims=True)
    top_rows = (tops + 7) // 8 * 8
    picker_row = lax.broadcasted_iota(jnp.int32, (top_rows, devices), 0)
    picker_rank = lax.broadcasted_iota(jnp.int32, (top_rows, devices), 1)
    parent_of = (
        picker_rank // strides[0] // 2 * top_strides[0]
        + picker_rank // strides[1] % numbers[1] // 2 * top_strides[1]
        + picker_rank % numbers[2] // 2
    )
    picker = (picker_row == parent_of).astype(F32)
    merged = lax.dot_general(
        picker, lifted, NN, precision=lax.Precision.HIGHEST, preferred_element_type=F32
    )
    merged = jnp.concatenate([merged, jnp.zeros((top_rows, LANES - terms), F32)], axis=1)
    uppers[devices : devices + top_rows, :] = merged

    def paired(value, line):
        value = jnp.broadcast_to(value, (8, LANES))
        upper = value.astype(BF16).astype(F32)
        lower = (value - upper).astype(BF16).astype(F32)
        page = jnp.where(row8 == line, upper, jnp.where(row8 == line + 1, lower, 0.0))
        return third(page)

    def fill_uppers(entry, carry):
        for kind, value in enumerate(paired(uppers[pl.ds(entry, 1), :], 0)):
            upper_pages[kind, entry] = value
        return carry

    lax.fori_loop(0, devices, fill_uppers, 0, unroll=4)

    def fill_tops(entry, carry):
        for kind, value in enumerate(paired(uppers[pl.ds(devices + entry, 1), :], 2)):
            top_pages[kind, entry] = value
        return carry

    lax.fori_loop(0, tops, fill_tops, 0)
    for kind in range(3):
        upper_pages[kind, devices] = jnp.zeros((8, LANES), F32)
        top_pages[kind, tops] = jnp.zeros((8, LANES), F32)

    lane16 = lax.broadcasted_iota(jnp.int32, (16, LANES), 1)
    first_part = lane16 < terms
    second_part = lane16 < 2 * terms - LANES

    def far_rows(triple):
        plans = [(3 * triple + kind) * PLAN for kind in range(3)]

        def tiles(held):
            return jnp.concatenate(
                [
                    jnp.where(first_part, held[0], held[1]),
                    jnp.where(second_part, held[1], held[2]),
                ],
                axis=1,
            )

        found = []
        for z in range(block_z):
            spots = [plan_ref[start + z] for start in plans]
            for x in range(block_x // 2):
                found.append(tiles([leaf_pages[kind, spots[kind] + 2 * x] for kind in range(3)]))
        held = []
        for kind in range(3):
            page = [mid_pages[kind, plan_ref[plans[kind] + 4 + entry]] for entry in range(4)]
            low = jnp.where(row8 < 4, page[0], page[1])
            high = jnp.where(row8 < 4, page[2], page[3])
            held.append(jnp.concatenate([low, high], axis=0).astype(BF16))
        found.append(tiles(held))
        held = []
        for kind in range(3):
            entries = [plan_ref[plans[kind] + 8 + axis] for axis in range(3)]
            upper = table[entries[0]] + table[8 + entries[1]] + table[16 + entries[2]]
            top = table[24 + entries[0]] + table[32 + entries[1]] + table[40 + entries[2]]
            page = upper_pages[kind, jnp.minimum(upper, devices)] + top_pages[kind, jnp.minimum(top, tops)]
            held.append(jnp.concatenate([page, jnp.zeros((8, LANES), F32)], axis=0).astype(BF16))
        found.append(tiles(held))
        return jnp.concatenate(found, axis=0)

    total_rows = 2 * leaves + 32
    sums[...] = jnp.zeros(sums.shape, F32)
    per_step = sources.shape[0] // LANES * SLOTS // STEPS

    def both_step(step, totals):
        products = []
        for which in range(GROUP):
            triple = step * GROUP + which
            products.append(
                lax.dot_general(
                    far_rows(triple),
                    operators[jnp.minimum(triple, used - 1)],
                    NT,
                    preferred_element_type=F32,
                )
            )
        sums[...] += (products[0] + products[2]) + (products[1] + products[3])
        sum_p, sum_x, sum_y, sum_z = totals
        first = step * per_step
        base = lax.div(first, SLOTS) * LANES + lax.rem(first, SLOTS)
        for line in range(per_step):
            s_x = sources[pl.ds(base + line, 1), :]
            s_y = sources[pl.ds(base + line + SLOTS, 1), :]
            s_z = sources[pl.ds(base + line + 2 * SLOTS, 1), :]
            s_q = sources[pl.ds(base + line + 3 * SLOTS, 1), :]
            d_x = targets[:SLOTS] - s_x
            d_y = targets[SLOTS : 2 * SLOTS] - s_y
            d_z = targets[2 * SLOTS : 3 * SLOTS] - s_z
            inverse = lax.rsqrt(d_x * d_x + d_y * d_y + d_z * d_z + SOFTENING)
            weight = s_q * inverse
            sum_p = sum_p + weight
            cubic = weight * (inverse * inverse)
            sum_x = sum_x + cubic * d_x
            sum_y = sum_y + cubic * d_y
            sum_z = sum_z + cubic * d_z
        return sum_p, sum_x, sum_y, sum_z

    zero = jnp.zeros((SLOTS, LANES), F32)
    near = lax.fori_loop(0, STEPS, both_step, (zero, zero, zero, zero))

    staged[5].wait()
    staged[6].wait()
    rows_from(down_raw, down_rows)
    first = 2 * leaves + 16
    held = sums[first : first + 8, :terms]
    far_upper = held[0:1] + held[1:2]
    far_top = held[2:3] + held[3:4]

    def lattice_apply(value):
        return apply(jnp.broadcast_to(value, (8, terms)), lattice[...])

    def wider(value):
        return jnp.concatenate([value, jnp.zeros((value.shape[0], LANES - terms), F32)], axis=1)

    top_local = 0.125 * (far_top + lattice_apply(root)[:1])
    octant = lax.rem(at[0], 2) * 4 + lax.rem(at[1], 2) * 2 + lax.rem(at[2], 2)
    moved = apply(jnp.broadcast_to(wider(top_local), (8, LANES)), octant_of(down_rows, octant))
    upper_local = jnp.broadcast_to(wider(0.25 * far_upper + moved[:1]), (8, LANES))
    mid_row = lax.broadcasted_iota(jnp.int32, (8, terms), 0)
    mid_octant = 4 * (mid_row // 2 % 2) + 2 * (mid_row % 2) + mid_row // 4
    held = sums[2 * leaves : 2 * leaves + 16, :terms]
    lines = []
    for z in range(2):
        for x in range(2):
            start = x * 8 + z * 4
            lines.append(held[start : start + 2] + held[start + 2 : start + 4])
    far_mid = jnp.concatenate(lines, axis=0)
    downward = [octant_of(down_rows, entry) for entry in range(8)]
    moved = jnp.zeros((8, terms), F32)
    for entry in range(8):
        moved = jnp.where(mid_octant == entry, apply(upper_local, downward[entry]), moved)
    mid_local = wider(0.5 * far_mid + moved)
    expanded = []
    for z in range(block_z):
        for x in range(block_x // 2):
            line = (z // 2 * 2 + x) * 2
            low = jnp.broadcast_to(mid_local[line : line + 1], (8, LANES))
            high = jnp.broadcast_to(mid_local[line + 1 : line + 2], (8, LANES))
            expanded.append(jnp.where(row8 % 4 < 2, low, high))
    expanded = jnp.concatenate(expanded, axis=0)
    moved = jnp.zeros((leaves, terms), F32)
    for entry in range(8):
        moved = jnp.where(leaf_octant == entry, apply(expanded, downward[entry]), moved)
    row_t = lax.broadcasted_iota(jnp.int32, (8, terms), 0)
    lines = []
    for spot in range(leaves // 8):
        low = sums[spot * 16 : spot * 16 + 8, :terms]
        high = sums[spot * 16 + 8 : spot * 16 + 16, :terms]
        low = low + pltpu.roll(low, 4, 0)
        high = high + pltpu.roll(high, 4, 0)
        lines.append(jnp.where(row_t < 4, low, high))
    local = wider(moved + jnp.concatenate(lines, axis=0))
    local_rows[...] = jnp.concatenate([local, local], axis=0).T

    u_x = targets[:SLOTS] - 0.5
    u_y = targets[SLOTS : 2 * SLOTS] - 0.5
    u_z = targets[2 * SLOTS : 3 * SLOTS] - 0.5
    value = grad_x = grad_y = grad_z = None
    for a in range(ORDER, -1, -1):
        inner = inner_y = inner_z = None
        for b in range(ORDER - a, -1, -1):
            here = local_rows[ROW_OF[(a, b, 0)] : ROW_OF[(a, b, 0)] + 1, :]
            if (a, b, 1) in ROW_OF:
                above = local_rows[ROW_OF[(a, b, 1)] : ROW_OF[(a, b, 1)] + 1, :]
                both = here + above * u_z
                inner_z = above if inner_z is None else inner_z * u_y + above
            else:
                both = here
            if inner is None:
                inner = jnp.broadcast_to(both, (SLOTS, LANES))
            else:
                inner_y = inner if inner_y is None else inner_y * u_y + inner
                inner = inner * u_y + both
        if value is None:
            value, grad_y, grad_z = inner, inner_y, inner_z
        else:
            grad_x = value if grad_x is None else grad_x * u_x + value
            value = value * u_x + inner
            if inner_y is not None:
                grad_y = inner_y if grad_y is None else grad_y * u_x + inner_y
            if inner_z is not None:
                grad_z = inner_z if grad_z is None else grad_z * u_x + inner_z

    def halves(total):
        return total + pltpu.roll(total, leaves, 1)

    self_term = targets[3 * SLOTS :] * (SOFTENING**-0.5)
    results = [
        halves(near[0]) - self_term + value,
        halves(near[1]) - grad_x,
        halves(near[2]) - grad_y,
        halves(near[3]) - grad_z,
    ]
    turned = jnp.concatenate(results, axis=0).T
    for entry in range(4):
        made = None
        for z in range(block_z):
            turn = (z - entry) * SLOTS % LANES
            held = turned[z * columns : (z + 1) * columns]
            held = pltpu.roll(held, turn, 1) if turn else held
            made = held if made is None else jnp.where(group == z, held, made)
        made = made * live
        for x in range(block_x):
            piece = made[x * block_y : (x + 1) * block_y]
            if entry == 0:
                potential_ref[x] = piece
            else:
                field_ref[entry - 1, x] = piece


def per_device(
    positions, charges, counts, moment_shift, far_operators, local_shift, lattice_operator
):
    block_x, block_y, column = charges.shape
    block_z = column // SLOTS
    sizes = (block_x, block_y, block_z)
    numbers = tuple(lax.axis_size(axis) for axis in ("gx", "gy", "gz"))
    devices = numbers[0] * numbers[1] * numbers[2]
    terms = moment_shift.shape[1]
    padded_terms = (terms + 15) // 16 * 16
    leaves = block_x * block_y * block_z
    plan, triples, none_leaf, none_mid, starts = plan_table(block_x, block_z)
    offsets = offset_table().shape[0]
    wide_x, wide_z = block_x + 2 * HALO, block_z + 2 * HALO
    wide_leaves = wide_x * wide_z * (block_y + 2 * HALO)
    mid_columns = (block_x // 2 + 4) * (block_z // 2 + 4)
    tops = devices // 8
    smem = pl.BlockSpec(memory_space=pltpu.SMEM)
    anywhere = pl.BlockSpec(memory_space=pl.ANY)
    vmem = pl.BlockSpec(memory_space=pltpu.VMEM)
    layout = (triples, none_leaf, none_mid, starts)
    potential, field_out = pl.pallas_call(
        lambda *refs: field_kernel(sizes, numbers, layout, *refs),
        out_shape=(
            jax.ShapeDtypeStruct((block_x, block_y, column), F32),
            jax.ShapeDtypeStruct((3, block_x, block_y, column), F32),
        ),
        in_specs=[smem] + [anywhere] * 7,
        out_specs=(vmem, vmem),
        scratch_shapes=[
            pltpu.VMEM(positions.shape, F32),
            pltpu.VMEM(charges.shape, F32),
            pltpu.VMEM(counts.shape, jnp.int32),
            pltpu.VMEM((terms, 8, terms), BF16),
            pltpu.VMEM((terms, far_operators.shape[1] + 2 * LANES), BF16),
            pltpu.VMEM((terms, 8, terms), BF16),
            pltpu.VMEM((terms, terms), BF16),
            pltpu.VMEM((block_y // 2 + 2, wide_z, wide_x, 2, LANES), F32),
            pltpu.VMEM((wide_leaves + 16, LANES), F32),
            pltpu.VMEM((4 * SLOTS, LANES), F32),
            pltpu.VMEM((padded_terms * 8, LANES), F32),
            pltpu.VMEM((wide_leaves + 16, LANES), F32),
            pltpu.VMEM((wide_leaves + 16, LANES), F32),
            pltpu.VMEM((devices * 8, LANES), F32),
            pltpu.VMEM((terms * 8, LANES), F32),
            pltpu.VMEM((terms * 8, LANES), F32),
            pltpu.VMEM((devices + (tops + 7) // 8 * 8, LANES), F32),
            pltpu.VMEM((-(-offsets // 3), padded_terms, 2 * LANES), BF16),
            pltpu.VMEM((14 * LANES, LANES), F32),
            pltpu.VMEM((3, none_leaf + 3, 16, LANES), BF16),
            pltpu.VMEM((mid_columns * 8 + 16, LANES), F32),
            pltpu.VMEM((mid_columns * 8 + 16, LANES), F32),
            pltpu.VMEM((3, none_mid + 1, 8, LANES), F32),
            pltpu.VMEM((3, devices + 1, 8, LANES), F32),
            pltpu.VMEM((3, tops + 1, 8, LANES), F32),
            pltpu.VMEM((2 * leaves + 32, padded_terms), F32),
            pltpu.VMEM((LANES, LANES), F32),
            pltpu.SMEM((48,), jnp.int32),
            pltpu.SemaphoreType.DMA((7,)),
            pltpu.SemaphoreType.DMA((27,)),
            pltpu.SemaphoreType.DMA((27,)),
            pltpu.SemaphoreType.DMA((devices,)),
            pltpu.SemaphoreType.DMA((devices,)),
        ],
        compiler_params=pltpu.CompilerParams(
            vmem_limit_bytes=60 * 1024 * 1024, collective_id=0, has_side_effects=True
        ),
        name="fields",
    )(
        jnp.asarray(plan),
        positions,
        charges,
        counts,
        jnp.transpose(moment_shift, (1, 0, 2)),
        far_operators,
        jnp.transpose(local_shift, (1, 0, 2)),
        lattice_operator,
    )
    return potential, field_out


def solution(mesh):
    placed = (
        P(None, "gx", "gy", "gz"),
        P("gx", "gy", "gz"),
        P("gx", "gy", "gz"),
        P(),
        P(),
        P(),
        P(),
    )
    return jax.shard_map(
        per_device,
        mesh=mesh,
        in_specs=placed,
        out_specs=(P("gx", "gy", "gz"), P(None, "gx", "gy", "gz")),
        check_vma=False,
    )
```

time: 86.3 us -> 41.7 us (0.48)
  Pallas kernels: 75 us -> 38.1 us
  other arithmetic: 6.03 us -> 0 us
  local copies, waits for them, and re-layouts: 4.33 us -> 2.64 us
    pallas_call x1, Pallas kernels: 75 us -> 38.1 us  [per_device(): pl.pallas_call(lambda *refs: field_kernel(sizes, numbers, layout, *refs),...]
    convert_element_type x2 -> x0, other arithmetic: 2.27 us -> none  [the longest x1 1.67 us: per_device(): (index[:, :, None] == jnp.arange(entries + top_count)[None, None, :]).ast...]
    select_n x3 -> x0, other arithmetic: 1.84 us -> none  [the longest x1 1.02 us: per_device(): jnp.where(jnp.arange(upper_rows)[None, :] == 0, picked[:, None], jnp.asar...]
    unnamed x15 -> x2, local copies, waits for them, and re-layouts: 4.08 us -> 2.64 us
where the time goes in v1:
time: 41.7 us; the launch traced here: 41.4 us
  Pallas kernels  38.1 us (91%)
  local copies, waits for them, and re-layouts  2.64 us (6%)
  between operations  0.64 us (2%)
    pallas_call x1, Pallas kernels, per_device(): pl.pallas_call(lambda *refs: field_kernel(sizes, numbers, layout, *refs),...  38.1 us
    unnamed x2, local copies, waits for them, and re-layouts  2.64 us

profile of v1, /device:TPU:0, one launch (start us, length us, event | category | flops | bytes accessed | tf_op | source)
XLA Modules:
  0.0 41.4 jit_solution(3879996931308958677)
XLA Ops:
  0.6 38.1 %fields.1 = (f32[4,4,128]{2,1,0:T(4,128)}, f32[3,4,4,128]{3,2,1,0:T(4,128)}) custom-call(s32[5376]{0:T(1024)} %constant.2.clone.refs_0_, f32[3,4,4,128]{3,2,1,0:T(4,128)} %refs_1_.1, f32[4,4,128]{2,1,0:T(4,128)} %refs_2_.1, s32[4,4,4]{2,1,0:T(4,128)} %refs_3_.1, bf16[81,8,81]{2,1,0:T(8,128)(2,1)} %bitcast.2, bf16[81,25600]{1,0:T(8,128)(2,1)} %refs_5_.1, ...), custom_call_target="tpu_custom_call" | custom-call | tf_op jit(solution)/shard_map/fields/pallas_call | solution.py:779
  38.7 1.3 %copy.12 = f32[4,4,128]{2,1,0:T(4,128)} copy(f32[4,4,128]{2,1,0:T(4,128)} %get-tuple-element.4) | data formatting | bytes 16384
  40.0 1.3 %copy.13 = f32[3,4,4,128]{3,2,1,0:T(4,128)} copy(f32[3,4,4,128]{3,2,1,0:T(4,128)} %get-tuple-element.5) | data formatting | bytes 49152

commit v2 on v1

--- a/solution.py
+++ b/solution.py
@@ -15,9 +15,10 @@
 BF16 = jnp.bfloat16
 NT = (((1,), (1,)), ((), ()))
 NN = (((1,), (0,)), ((), ()))
-PLAN = 16
+PLAN = 4
 GROUP = 4
 STEPS = 28
+PLACED = 9
 
 
 def offset_table():
@@ -74,33 +75,28 @@
 def plan_table(block_x, block_z):
     shifts = offset_table()
     wide_x, wide_z = block_x + 2 * HALO, block_z + 2 * HALO
-    starts = 2 * (wide_x - 1) // 2 + 4
+    starts = wide_x + 3
     triples = STEPS * GROUP
     assert 3 * triples >= shifts.shape[0]
     plan = np.zeros((triples * 3, PLAN), np.int32)
-    none_leaf = 7 * wide_z * starts
-    mid_x, mid_z = block_x // 2 + 4, block_z // 2 + 4
-    none_mid = 7 * mid_z * mid_x
-    plan[:, :4] = none_leaf
-    plan[:, 4:8] = none_mid
-    plan[:, 8:11] = 7
+    none = 7 * wide_z * starts
+    plan[:, :2] = none
+    plan[:, 2] = 49
+    plan[:, 3] = 7
     for row, (dx, dy, dz) in enumerate(shifts):
-        for z in range(block_z):
-            if admits(dz, z % 2):
+        for z in range(2):
+            if admits(dz, z):
                 plan[row, z] = ((dy + 3) * wide_z + z + 2 + dz) * starts + leaf_start(dx)
-        for x in range(2):
-            for z in range(2):
-                if admits(dz, z) and admits(dx, x):
-                    plan[row, 4 + x * 2 + z] = ((dy + 3) * mid_z + z + 2 + dz) * mid_x + x + 2 + dx
-        plan[row, 8:11] = (dx + 3, dy + 3, dz + 3)
-    return plan.reshape(-1), triples, none_leaf, none_mid, starts
+        plan[row, 2] = (dx + 3) * 7 + dy + 3
+        plan[row, 3] = dz + 3
+    return plan.reshape(-1), triples, none, starts
 
 
 def field_kernel(
     sizes,
     numbers,
     layout,
-    plan_ref,
+    plan_hbm,
     positions_hbm,
     charges_hbm,
     counts_hbm,
@@ -129,15 +125,15 @@
     uppers,
     operators,
     sources,
-    leaf_pages,
+    pages,
     mid_high,
     mid_low,
-    mid_pages,
     upper_pages,
-    top_pages,
     sums,
     local_rows,
+    plan_ref,
     table,
+    reach,
     loads,
     sends,
     receives,
@@ -145,7 +141,7 @@
     mid_receive,
 ):
     block_x, block_y, block_z = sizes
-    triples, none_leaf, none_mid, starts = layout
+    triples, none, starts = layout
     wide_x, wide_z = block_x + 2 * HALO, block_z + 2 * HALO
     rows_y = block_y + 2 * HALO
     columns = block_x * block_y
@@ -158,13 +154,8 @@
     rank = (at[0] * numbers[1] + at[1]) * numbers[2] + at[2]
     barrier = pltpu.get_barrier_semaphore()
 
-    def coordinates(step):
-        other = lax.rem(rank + step, devices)
-        return (
-            lax.div(other, numbers[1] * numbers[2]),
-            lax.rem(lax.div(other, numbers[2]), numbers[1]),
-            lax.rem(other, numbers[2]),
-        )
+    def other(step):
+        return lax.rem(rank + step, devices)
 
     staged = [
         pltpu.make_async_copy(positions_hbm, positions, loads.at[0]),
@@ -174,13 +165,14 @@
         pltpu.make_async_copy(far_hbm, far.at[:, pl.ds(0, far_hbm.shape[1])], loads.at[4]),
         pltpu.make_async_copy(down_hbm, down_raw, loads.at[5]),
         pltpu.make_async_copy(lattice_hbm, lattice, loads.at[6]),
+        pltpu.make_async_copy(plan_hbm, plan_ref, loads.at[7]),
     ]
     for copy in staged:
         copy.start()
 
     def greet(step, carry):
         pl.semaphore_signal(
-            barrier, inc=1, device_id=coordinates(step), device_id_type=pl.DeviceIdType.MESH
+            barrier, inc=1, device_id=other(step), device_id_type=pl.DeviceIdType.LOGICAL
         )
         return carry
 
@@ -316,8 +308,8 @@
             dst_ref=own_slot,
             send_sem=mid_send.at[step],
             recv_sem=mid_receive.at[step],
-            device_id=coordinates(step),
-            device_id_type=pl.DeviceIdType.MESH,
+            device_id=other(step),
+            device_id_type=pl.DeviceIdType.LOGICAL,
         )
 
     def send_mid(step, carry):
@@ -329,58 +321,98 @@
         return carry
 
     lax.fori_loop(1, devices, send_mid, 0)
-
-    staged[4].wait()
-    far[:, pl.ds(far_hbm.shape[1], 2 * LANES)] = jnp.zeros((terms, 2 * LANES), BF16)
-    tall = lax.broadcasted_iota(jnp.int32, (padded_terms, LANES), 1)
-
-    def place(triple, carry):
-        start = triple * (3 * terms)
-        turn = lax.rem(start, LANES)
-        base = pl.multiple_of(start - turn, LANES)
-        back = lax.rem(LANES - turn, LANES)
-        turned = []
-        for tile in range(3):
-            held = far[:, pl.ds(pl.multiple_of(base + tile * LANES, LANES), LANES)].astype(F32)
-            held = jnp.concatenate([held, jnp.zeros((padded_terms - terms, LANES), F32)], axis=0)
-            turned.append(pltpu.roll(held, back, 1))
-        kept = tall < LANES - turn
-        for tile in range(2):
-            found = jnp.where(kept, turned[tile], turned[tile + 1])
-            operators[triple, :, tile * LANES : (tile + 1) * LANES] = found.astype(BF16)
-        return carry
-
-    used = operators.shape[0]
-    lax.fori_loop(0, used, place, 0, unroll=2)
 
     strides = (numbers[1] * numbers[2], numbers[2], 1)
     top_sizes = tuple(number // 2 for number in numbers)
     top_strides = (top_sizes[1] * top_sizes[2], top_sizes[2], 1)
     tops = devices // 8
+    spots, top_spots = [], []
     for axis in range(3):
         odd = lax.rem(at[axis], 2)
+        listed, top_listed = [], []
         for entry in range(7):
             shift = entry - 3
             size = numbers[axis]
-            place_at = lax.rem(at[axis] + shift + 4 * size, size) * strides[axis]
+            spot = lax.rem(at[axis] + shift + 4 * size, size) * strides[axis]
             if shift == -3:
-                place_at = jnp.where(odd == 1, place_at, 4 * devices)
+                spot = jnp.where(odd == 1, spot, 4 * devices)
             if shift == 3:
-                place_at = jnp.where(odd == 0, place_at, 4 * devices)
-            table[axis * 8 + entry] = place_at
+                spot = jnp.where(odd == 0, spot, 4 * devices)
+            listed.append(spot)
             size = top_sizes[axis]
-            table[24 + axis * 8 + entry] = (
+            top_listed.append(
                 lax.rem(lax.div(at[axis], 2) + shift + 4 * size, size) * top_strides[axis]
             )
-        table[axis * 8 + 7] = jnp.int32(4 * devices)
-        table[24 + axis * 8 + 7] = jnp.int32(4 * devices)
+        spots.append(listed)
+        top_spots.append(top_listed)
+    for x in range(7):
+        for y in range(7):
+            table[0, x * 7 + y] = spots[0][x] + spots[1][y]
+            table[1, x * 7 + y] = top_spots[0][x] + top_spots[1][y]
+    for z in range(7):
+        table[2, z] = spots[2][z]
+        table[3, z] = top_spots[2][z]
+    for line, entry in ((0, 49), (1, 49), (2, 7), (3, 7)):
+        table[line, entry] = jnp.int32(4 * devices)
+    staged[7].wait()
+
+    def reach_of(row):
+        level, depth = plan_ref[row * PLAN + 2], plan_ref[row * PLAN + 3]
+        reach[2 * row] = jnp.minimum(table[0, level] + table[2, depth], devices)
+        reach[2 * row + 1] = jnp.minimum(table[1, level] + table[3, depth], tops) + devices + 1
+
+    staged[4].wait()
+    spare_width = far.shape[1] - far_hbm.shape[1]
+    far[:, pl.ds(far_hbm.shape[1], spare_width)] = jnp.zeros((terms, spare_width), BF16)
+    tall = lax.broadcasted_iota(jnp.int32, (padded_terms, LANES), 1)
+    spare_rows = jnp.zeros((padded_terms - terms, LANES), BF16)
+
+    def place(batch, carry):
+        for local in range(2 * PLACED):
+            triple = batch * (2 * PLACED) + local
+            start = triple * (3 * terms)
+            turn = lax.rem(start, LANES)
+            base = pl.multiple_of(start - turn, LANES)
+            back = lax.rem(LANES - turn, LANES)
+            turned = []
+            for tile in range(3):
+                held = far[:, pl.ds(pl.multiple_of(base + tile * LANES, LANES), LANES)]
+                turned.append(pltpu.roll(jnp.concatenate([held, spare_rows], axis=0), back, 1))
+            kept = tall < LANES - turn
+            for tile in range(2):
+                found = jnp.where(kept, turned[tile], turned[tile + 1])
+                spot = (local % 2) * 2 + tile
+                operators[
+                    batch * PLACED + local // 2, :, spot * LANES : (spot + 1) * LANES
+                ] = found
+            for kind in range(3):
+                reach_of(3 * triple + kind)
+        return carry
+
+    used = operators.shape[0]
+    lax.fori_loop(0, used // PLACED, place, 0)
+    for row in range(used * 6, triples * 3):
+        reach_of(row)
 
     for copy in copies:
         copy.wait()
     guard = 8
-    for ref in (wide, moments_high, moments_low):
+
+    def clear(ref):
         ref[:guard, :] = jnp.zeros((guard, LANES), F32)
         ref[ref.shape[0] - guard :, :] = jnp.zeros((guard, LANES), F32)
+
+    clear(wide)
+    for kind in range(3):
+        for ref in (moments_high, moments_low, mid_high, mid_low):
+            clear(ref.at[kind])
+
+    def third(value):
+        return (value, pltpu.roll(value, terms, 1), pltpu.roll(value, 2 * terms - LANES, 1))
+
+    def halved(value):
+        upper = value.astype(BF16).astype(F32)
+        return upper, (value - upper).astype(BF16).astype(F32)
 
     def widen(z, carry):
         for x in range(wide_x):
@@ -396,9 +428,10 @@
         found = moments(
             turned[:SLOTS], turned[SLOTS : 2 * SLOTS], turned[2 * SLOTS : 3 * SLOTS], turned[3 * SLOTS :]
         )
-        upper = found.astype(BF16).astype(F32)
-        moments_high[pl.ds(start, LANES), :] = upper
-        moments_low[pl.ds(start, LANES), :] = (found - upper).astype(BF16).astype(F32)
+        for kind, value in enumerate(third(found)):
+            upper, lower = halved(value)
+            moments_high[kind, pl.ds(start, LANES), :] = upper
+            moments_low[kind, pl.ds(start, LANES), :] = lower
         return carry
 
     lax.fori_loop(0, wide_x * wide_z * rows_y // LANES, window, 0)
@@ -431,48 +464,43 @@
             second = [jnp.where(group8 < 3, value, 0.0) for value in first]
         sources[pair * LANES : (pair + 1) * LANES, :] = jnp.concatenate(first + second, axis=0).T
 
-    def third(value):
-        return (value, pltpu.roll(value, terms, 1), pltpu.roll(value, 2 * terms - LANES, 1))
-
     odd_line = row8 % 2 == 1
+    zero8 = jnp.zeros((8, LANES), F32)
+
+    def parity(page, shift):
+        if shift == -3:
+            return jnp.where(odd_line, page, 0.0)
+        if shift == 3:
+            return jnp.where(odd_line, 0.0, page)
+        return page
 
     def fill_pages(z, carry):
         for shift in range(-3, 4):
-            turned = []
-            for x in range(wide_x):
-                start = guard + (z * wide_x + x) * rows_y + HALO + shift
-                page = jnp.where(
-                    row8 < block_y,
-                    moments_high[pl.ds(start, 8), :],
-                    moments_low[pl.ds(start - block_y, 8), :],
-                )
-                if shift == -3:
-                    page = jnp.where(odd_line, page, 0.0)
-                if shift == 3:
-                    page = jnp.where(odd_line, 0.0, page)
-                turned.append(third(page))
             spot = ((shift + 3) * wide_z + z) * starts
-            zero = jnp.zeros((8, LANES), F32)
             for kind in range(3):
-                listed = [(x, turned[x][kind], turned[x + 1][kind]) for x in range(wide_x - 1)]
-                listed.append((7, zero, turned[0][kind]))
-                listed.append((9, zero, turned[2][kind]))
-                listed.append((8, turned[5][kind], zero))
-                listed.append((10, turned[7][kind], zero))
+                made = []
+                for x in range(wide_x):
+                    start = guard + (z * wide_x + x) * rows_y + HALO + shift
+                    page = jnp.where(
+                        row8 < block_y,
+                        moments_high[kind, pl.ds(start, 8), :],
+                        moments_low[kind, pl.ds(start - block_y, 8), :],
+                    )
+                    made.append(parity(page, shift))
+                listed = [(x, made[x], made[x + 1]) for x in range(wide_x - 1)]
+                listed += [(7, zero8, made[0]), (9, zero8, made[2])]
+                listed += [(8, made[5], zero8), (10, made[7], zero8)]
                 for entry, low, high in listed:
-                    leaf_pages[kind, spot + entry] = jnp.concatenate([low, high], axis=0).astype(BF16)
+                    pages[kind, spot + entry] = jnp.concatenate([low, high], axis=0).astype(BF16)
         return carry
 
     lax.fori_loop(0, wide_z, fill_pages, 0)
-    for kind in range(3):
-        for entry in range(3):
-            leaf_pages[kind, none_leaf + entry] = jnp.zeros((16, LANES), BF16)
+    for kind in range(6):
+        for entry in range(pages.shape[1] - none):
+            pages[kind, none + entry] = jnp.zeros((16, LANES), BF16)
 
     lax.fori_loop(1, devices, wait_mid, 0)
     mid_x, mid_z = block_x // 2 + 4, block_z // 2 + 4
-    for ref in (mid_high, mid_low):
-        ref[:guard, :] = jnp.zeros((guard, LANES), F32)
-        ref[ref.shape[0] - guard :, :] = jnp.zeros((guard, LANES), F32)
     around = []
     for count in range(27):
         moves = (count // 9 - 1, count // 3 % 3 - 1, count % 3 - 1)
@@ -487,38 +515,40 @@
                 listed.append(mids[pl.ds(base + line, 2), :])
             listed.append(jnp.zeros((2, LANES), F32))
             held = jnp.concatenate(listed, axis=0)
-            upper = held.astype(BF16).astype(F32)
             start = guard + (z * mid_x + x) * 8
-            mid_high[start : start + 8, :] = upper
-            mid_low[start : start + 8, :] = (held - upper).astype(BF16).astype(F32)
+            for kind, value in enumerate(third(held)):
+                upper, lower = halved(value)
+                mid_high[kind, start : start + 8, :] = upper
+                mid_low[kind, start : start + 8, :] = lower
 
     def fill_mids(z, carry):
-        for x in range(mid_x):
-            for shift in range(-3, 4):
-                start = guard + (z * mid_x + x) * 8 + 2 + shift
-                page = jnp.where(
-                    row8 < 4,
-                    jnp.where(row8 < 2, mid_high[pl.ds(start, 8), :], mid_low[pl.ds(start - 2, 8), :]),
-                    jnp.where(row8 < 6, mid_high[pl.ds(start - 4, 8), :], mid_low[pl.ds(start - 6, 8), :]),
-                )
-                if shift == -3:
-                    page = jnp.where(odd_line, page, 0.0)
-                if shift == 3:
-                    page = jnp.where(odd_line, 0.0, page)
-                for kind, value in enumerate(third(page)):
-                    mid_pages[kind, ((shift + 3) * mid_z + z) * mid_x + x] = value
+        for shift in range(-3, 4):
+            spot = ((shift + 3) * wide_z + z) * starts
+            for kind in range(3):
+                made = []
+                for x in range(mid_x):
+                    start = guard + (z * mid_x + x) * 8 + 2 + shift
+                    page = jnp.where(
+                        row8 < 2,
+                        mid_high[kind, pl.ds(start, 8), :],
+                        mid_low[kind, pl.ds(start - 2, 8), :],
+                    )
+                    made.append(parity(page, shift))
+                moved = [pltpu.roll(page, 4, 0) for page in made]
+                listed = [(x, made[x], moved[x + 1]) for x in range(mid_x - 1)]
+                listed += [(7, zero8, moved[0]), (8, made[5], zero8)]
+                for entry, low, high in listed:
+                    page = jnp.where(row8 < 4, low, high)
+                    pages[3 + kind, spot + entry] = jnp.concatenate([page, page], axis=0).astype(BF16)
         return carry
 
     lax.fori_loop(0, mid_z, fill_mids, 0)
-    for kind in range(3):
-        mid_pages[kind, none_mid] = jnp.zeros((8, LANES), F32)
 
     raised = jnp.zeros((devices, terms), F32)
     for octant in range(8):
         line = (octant % 2 * 2 + octant // 4) * 2 + octant // 2 % 2
         raised = raised + apply(mids[pl.ds(line, devices, stride=8), :], octant_of(shift_rows, octant))
     raised = jnp.concatenate([raised, jnp.zeros((devices, LANES - terms), F32)], axis=1)
-    uppers[:devices, :] = raised
     rank_row = lax.broadcasted_iota(jnp.int32, (devices, terms), 0)
     rank_octant = (
         4 * (rank_row // strides[0] % 2) + 2 * (rank_row // strides[1] % 2) + rank_row % 2
@@ -541,38 +571,37 @@
         picker, lifted, NN, precision=lax.Precision.HIGHEST, preferred_element_type=F32
     )
     merged = jnp.concatenate([merged, jnp.zeros((top_rows, LANES - terms), F32)], axis=1)
-    uppers[devices : devices + top_rows, :] = merged
-
-    def paired(value, line):
-        value = jnp.broadcast_to(value, (8, LANES))
-        upper = value.astype(BF16).astype(F32)
-        lower = (value - upper).astype(BF16).astype(F32)
-        page = jnp.where(row8 == line, upper, jnp.where(row8 == line + 1, lower, 0.0))
-        return third(page)
-
-    def fill_uppers(entry, carry):
-        for kind, value in enumerate(paired(uppers[pl.ds(entry, 1), :], 0)):
-            upper_pages[kind, entry] = value
-        return carry
-
-    lax.fori_loop(0, devices, fill_uppers, 0, unroll=4)
-
-    def fill_tops(entry, carry):
-        for kind, value in enumerate(paired(uppers[pl.ds(devices + entry, 1), :], 2)):
-            top_pages[kind, entry] = value
-        return carry
-
-    lax.fori_loop(0, tops, fill_tops, 0)
+    for kind, value in enumerate(third(jnp.concatenate([raised, merged], axis=0))):
+        upper, lower = halved(value)
+        uppers[2 * kind] = upper
+        uppers[2 * kind + 1] = lower
+
+    def fill_uppers(line):
+        def fill(entry, carry):
+            for kind in range(3):
+                high = jnp.broadcast_to(uppers[2 * kind, pl.ds(line[1] + entry, 1), :], (8, LANES))
+                low = jnp.broadcast_to(uppers[2 * kind + 1, pl.ds(line[1] + entry, 1), :], (8, LANES))
+                page = jnp.where(row8 == line[0], high, jnp.where(row8 == line[0] + 1, low, 0.0))
+                upper_pages[kind, line[2] + entry] = jnp.concatenate([page, zero8], axis=0).astype(BF16)
+            return carry
+
+        return fill
+
+    lax.fori_loop(0, devices, fill_uppers((0, 0, 0)), 0, unroll=8)
+    lax.fori_loop(0, tops, fill_uppers((2, devices, devices + 1)), 0, unroll=4)
     for kind in range(3):
-        upper_pages[kind, devices] = jnp.zeros((8, LANES), F32)
-        top_pages[kind, tops] = jnp.zeros((8, LANES), F32)
+        upper_pages[kind, devices] = jnp.zeros((16, LANES), BF16)
+        upper_pages[kind, devices + 1 + tops] = jnp.zeros((16, LANES), BF16)
 
     lane16 = lax.broadcasted_iota(jnp.int32, (16, LANES), 1)
     first_part = lane16 < terms
     second_part = lane16 < 2 * terms - LANES
 
+    first_eight = lax.broadcasted_iota(jnp.int32, (16, LANES), 0) < 8
+
     def far_rows(triple):
-        plans = [(3 * triple + kind) * PLAN for kind in range(3)]
+        rows = [3 * triple + kind for kind in range(3)]
+        spots = [[plan_ref[row * PLAN + odd] for odd in range(2)] for row in rows]
 
         def tiles(held):
             return jnp.concatenate(
@@ -585,23 +614,17 @@
 
         found = []
         for z in range(block_z):
-            spots = [plan_ref[start + z] for start in plans]
             for x in range(block_x // 2):
-                found.append(tiles([leaf_pages[kind, spots[kind] + 2 * x] for kind in range(3)]))
+                step = z // 2 * 2 * starts + 2 * x
+                found.append(tiles([pages[kind, spots[kind][z % 2] + step] for kind in range(3)]))
         held = []
         for kind in range(3):
-            page = [mid_pages[kind, plan_ref[plans[kind] + 4 + entry]] for entry in range(4)]
-            low = jnp.where(row8 < 4, page[0], page[1])
-            high = jnp.where(row8 < 4, page[2], page[3])
-            held.append(jnp.concatenate([low, high], axis=0).astype(BF16))
+            even, odd = pages[3 + kind, spots[kind][0]], pages[3 + kind, spots[kind][1]]
+            held.append(jnp.where(first_eight, even, odd))
         found.append(tiles(held))
         held = []
-        for kind in range(3):
-            entries = [plan_ref[plans[kind] + 8 + axis] for axis in range(3)]
-            upper = table[entries[0]] + table[8 + entries[1]] + table[16 + entries[2]]
-            top = table[24 + entries[0]] + table[32 + entries[1]] + table[40 + entries[2]]
-            page = upper_pages[kind, jnp.minimum(upper, devices)] + top_pages[kind, jnp.minimum(top, tops)]
-            held.append(jnp.concatenate([page, jnp.zeros((8, LANES), F32)], axis=0).astype(BF16))
+        for kind, row in enumerate(rows):
+            held.append(upper_pages[kind, reach[2 * row]] + upper_pages[kind, reach[2 * row + 1]])
         found.append(tiles(held))
         return jnp.concatenate(found, axis=0)
 
@@ -611,17 +634,18 @@
 
     def both_step(step, totals):
         products = []
-        for which in range(GROUP):
-            triple = step * GROUP + which
+        for which in range(GROUP // 2):
+            pair = step * (GROUP // 2) + which
+            left = jnp.concatenate([far_rows(2 * pair), far_rows(2 * pair + 1)], axis=1)
             products.append(
                 lax.dot_general(
-                    far_rows(triple),
-                    operators[jnp.minimum(triple, used - 1)],
+                    left,
+                    operators[jnp.minimum(pair, used - 1)],
                     NT,
                     preferred_element_type=F32,
                 )
             )
-        sums[...] += (products[0] + products[2]) + (products[1] + products[3])
+        sums[...] += products[0] + products[1]
         sum_p, sum_x, sum_y, sum_z = totals
         first = step * per_step
         base = lax.div(first, SLOTS) * LANES + lax.rem(first, SLOTS)
@@ -669,7 +693,7 @@
     lines = []
     for z in range(2):
         for x in range(2):
-            start = x * 8 + z * 4
+            start = z * 8 + x * 4
             lines.append(held[start : start + 2] + held[start + 2 : start + 4])
     far_mid = jnp.concatenate(lines, axis=0)
     downward = [octant_of(down_rows, entry) for entry in range(8)]
@@ -766,54 +790,57 @@
     terms = moment_shift.shape[1]
     padded_terms = (terms + 15) // 16 * 16
     leaves = block_x * block_y * block_z
-    plan, triples, none_leaf, none_mid, starts = plan_table(block_x, block_z)
+    plan, triples, none, starts = plan_table(block_x, block_z)
     offsets = offset_table().shape[0]
     wide_x, wide_z = block_x + 2 * HALO, block_z + 2 * HALO
     wide_leaves = wide_x * wide_z * (block_y + 2 * HALO)
     mid_columns = (block_x // 2 + 4) * (block_z // 2 + 4)
     tops = devices // 8
-    smem = pl.BlockSpec(memory_space=pltpu.SMEM)
     anywhere = pl.BlockSpec(memory_space=pl.ANY)
     vmem = pl.BlockSpec(memory_space=pltpu.VMEM)
-    layout = (triples, none_leaf, none_mid, starts)
+    layout = (triples, none, starts)
+    batches = -(-offsets // (6 * PLACED))
+    top_rows = (tops + 7) // 8 * 8
+    placed = batches * PLACED
+    spare = (placed * 6 * terms + 2 * LANES - far_operators.shape[1] + LANES) // LANES * LANES
     potential, field_out = pl.pallas_call(
         lambda *refs: field_kernel(sizes, numbers, layout, *refs),
         out_shape=(
             jax.ShapeDtypeStruct((block_x, block_y, column), F32),
             jax.ShapeDtypeStruct((3, block_x, block_y, column), F32),
         ),
-        in_specs=[smem] + [anywhere] * 7,
+        in_specs=[anywhere] * 8,
         out_specs=(vmem, vmem),
         scratch_shapes=[
             pltpu.VMEM(positions.shape, F32),
             pltpu.VMEM(charges.shape, F32),
             pltpu.VMEM(counts.shape, jnp.int32),
             pltpu.VMEM((terms, 8, terms), BF16),
-            pltpu.VMEM((terms, far_operators.shape[1] + 2 * LANES), BF16),
+            pltpu.VMEM((terms, far_operators.shape[1] + spare), BF16),
             pltpu.VMEM((terms, 8, terms), BF16),
             pltpu.VMEM((terms, terms), BF16),
             pltpu.VMEM((block_y // 2 + 2, wide_z, wide_x, 2, LANES), F32),
             pltpu.VMEM((wide_leaves + 16, LANES), F32),
             pltpu.VMEM((4 * SLOTS, LANES), F32),
             pltpu.VMEM((padded_terms * 8, LANES), F32),
-            pltpu.VMEM((wide_leaves + 16, LANES), F32),
-            pltpu.VMEM((wide_leaves + 16, LANES), F32),
+            pltpu.VMEM((3, wide_leaves + 16, LANES), F32),
+            pltpu.VMEM((3, wide_leaves + 16, LANES), F32),
             pltpu.VMEM((devices * 8, LANES), F32),
             pltpu.VMEM((terms * 8, LANES), F32),
             pltpu.VMEM((terms * 8, LANES), F32),
-            pltpu.VMEM((devices + (tops + 7) // 8 * 8, LANES), F32),
-            pltpu.VMEM((-(-offsets // 3), padded_terms, 2 * LANES), BF16),
+            pltpu.VMEM((6, devices + top_rows, LANES), F32),
+            pltpu.VMEM((placed, padded_terms, 4 * LANES), BF16),
             pltpu.VMEM((14 * LANES, LANES), F32),
-            pltpu.VMEM((3, none_leaf + 3, 16, LANES), BF16),
-            pltpu.VMEM((mid_columns * 8 + 16, LANES), F32),
-            pltpu.VMEM((mid_columns * 8 + 16, LANES), F32),
-            pltpu.VMEM((3, none_mid + 1, 8, LANES), F32),
-            pltpu.VMEM((3, devices + 1, 8, LANES), F32),
-            pltpu.VMEM((3, tops + 1, 8, LANES), F32),
+            pltpu.VMEM((6, none + 2 * starts + 3, 16, LANES), BF16),
+            pltpu.VMEM((3, mid_columns * 8 + 16, LANES), F32),
+            pltpu.VMEM((3, mid_columns * 8 + 16, LANES), F32),
+            pltpu.VMEM((3, devices + tops + 2, 16, LANES), BF16),
             pltpu.VMEM((2 * leaves + 32, padded_terms), F32),
             pltpu.VMEM((LANES, LANES), F32),
-            pltpu.SMEM((48,), jnp.int32),
-            pltpu.SemaphoreType.DMA((7,)),
+            pltpu.SMEM(plan.shape, jnp.int32),
+            pltpu.SMEM((4, LANES), jnp.int32),
+            pltpu.SMEM((triples * 6,), jnp.int32),
+            pltpu.SemaphoreType.DMA((8,)),
             pltpu.SemaphoreType.DMA((27,)),
             pltpu.SemaphoreType.DMA((27,)),
             pltpu.SemaphoreType.DMA((devices,)),

time: 41.7 us -> 35.5 us (0.85)
  Pallas kernels: 38.1 us -> 32 us
    pallas_call x1, Pallas kernels: 38.1 us -> 32 us  [per_device(): pl.pallas_call(lambda *refs: field_kernel(sizes, numbers, layout, *refs),...]
where the time goes in v2:
time: 35.5 us; the launch traced here: 35.2 us
  Pallas kernels  32 us (90%)
  local copies, waits for them, and re-layouts  2.64 us (7%)
  between operations  0.64 us (2%)
    pallas_call x1, Pallas kernels, per_device(): pl.pallas_call(lambda *refs: field_kernel(sizes, numbers, layout, *refs),...  32 us
    unnamed x2, local copies, waits for them, and re-layouts  2.64 us

profile of v2, /device:TPU:0, one launch (start us, length us, event | category | flops | bytes accessed | tf_op | source)
XLA Modules:
  0.0 35.2 jit_solution(8729883735737811917)
XLA Ops:
  0.6 32.0 %fields.1 = (f32[4,4,128]{2,1,0:T(4,128)}, f32[3,4,4,128]{3,2,1,0:T(4,128)}) custom-call(s32[1344]{0:T(1024)} %constant.2.clone.refs_0_, f32[3,4,4,128]{3,2,1,0:T(4,128)} %refs_1_.1, f32[4,4,128]{2,1,0:T(4,128)} %refs_2_.1, s32[4,4,4]{2,1,0:T(4,128)} %refs_3_.1, bf16[81,8,81]{2,1,0:T(8,128)(2,1)} %bitcast.2, bf16[81,25600]{1,0:T(8,128)(2,1)} %refs_5_.1, ...), custom_call_target="tpu_custom_call" | custom-call | tf_op jit(solution)/shard_map/fields/pallas_call | solution.py:806
  32.6 1.3 %copy.12 = f32[4,4,128]{2,1,0:T(4,128)} copy(f32[4,4,128]{2,1,0:T(4,128)} %get-tuple-element.4) | data formatting | bytes 16384
  33.9 1.3 %copy.13 = f32[3,4,4,128]{3,2,1,0:T(4,128)} copy(f32[3,4,4,128]{3,2,1,0:T(4,128)} %get-tuple-element.5) | data formatting | bytes 49152

commit v3 on v2

--- a/solution.py
+++ b/solution.py
@@ -104,8 +104,7 @@
     far_hbm,
     down_hbm,
     lattice_hbm,
-    potential_ref,
-    field_ref,
+    result_ref,
     positions,
     charges,
     counts,
@@ -347,19 +346,19 @@
         top_spots.append(top_listed)
     for x in range(7):
         for y in range(7):
-            table[0, x * 7 + y] = spots[0][x] + spots[1][y]
-            table[1, x * 7 + y] = top_spots[0][x] + top_spots[1][y]
+            table[x * 7 + y] = spots[0][x] + spots[1][y]
+            table[LANES + x * 7 + y] = top_spots[0][x] + top_spots[1][y]
     for z in range(7):
-        table[2, z] = spots[2][z]
-        table[3, z] = top_spots[2][z]
+        table[2 * LANES + z] = spots[2][z]
+        table[3 * LANES + z] = top_spots[2][z]
     for line, entry in ((0, 49), (1, 49), (2, 7), (3, 7)):
-        table[line, entry] = jnp.int32(4 * devices)
+        table[line * LANES + entry] = jnp.int32(4 * devices)
     staged[7].wait()
 
     def reach_of(row):
         level, depth = plan_ref[row * PLAN + 2], plan_ref[row * PLAN + 3]
-        reach[2 * row] = jnp.minimum(table[0, level] + table[2, depth], devices)
-        reach[2 * row + 1] = jnp.minimum(table[1, level] + table[3, depth], tops) + devices + 1
+        reach[2 * row] = jnp.minimum(table[level] + table[2 * LANES + depth], devices)
+        reach[2 * row + 1] = jnp.minimum(table[LANES + level] + table[3 * LANES + depth], tops) + devices + 1
 
     staged[4].wait()
     spare_width = far.shape[1] - far_hbm.shape[1]
@@ -371,13 +370,14 @@
         for local in range(2 * PLACED):
             triple = batch * (2 * PLACED) + local
             start = triple * (3 * terms)
-            turn = lax.rem(start, LANES)
+            turn = start & (LANES - 1)
             base = pl.multiple_of(start - turn, LANES)
-            back = lax.rem(LANES - turn, LANES)
+            back = (LANES - turn) & (LANES - 1)
+            held = far[:, pl.ds(base, 3 * LANES)]
             turned = []
             for tile in range(3):
-                held = far[:, pl.ds(pl.multiple_of(base + tile * LANES, LANES), LANES)]
-                turned.append(pltpu.roll(jnp.concatenate([held, spare_rows], axis=0), back, 1))
+                piece = held[:, tile * LANES : (tile + 1) * LANES]
+                turned.append(pltpu.roll(jnp.concatenate([piece, spare_rows], axis=0), back, 1))
             kept = tall < LANES - turn
             for tile in range(2):
                 found = jnp.where(kept, turned[tile], turned[tile + 1])
@@ -434,7 +434,7 @@
             moments_low[kind, pl.ds(start, LANES), :] = lower
         return carry
 
-    lax.fori_loop(0, wide_x * wide_z * rows_y // LANES, window, 0)
+    lax.fori_loop(0, wide_x * wide_z * rows_y // LANES, window, 0, unroll=2)
 
     near_shifts = [(x, y, z) for x in (-1, 0, 1) for y in (-1, 0, 1) for z in (-1, 0, 1)]
     lane8 = lax.broadcasted_iota(jnp.int32, (8, LANES), 1)
@@ -630,22 +630,10 @@
 
     total_rows = 2 * leaves + 32
     sums[...] = jnp.zeros(sums.shape, F32)
-    per_step = sources.shape[0] // LANES * SLOTS // STEPS
+    near_steps = sources.shape[0] // LANES
+    per_step = SLOTS
 
     def both_step(step, totals):
-        products = []
-        for which in range(GROUP // 2):
-            pair = step * (GROUP // 2) + which
-            left = jnp.concatenate([far_rows(2 * pair), far_rows(2 * pair + 1)], axis=1)
-            products.append(
-                lax.dot_general(
-                    left,
-                    operators[jnp.minimum(pair, used - 1)],
-                    NT,
-                    preferred_element_type=F32,
-                )
-            )
-        sums[...] += products[0] + products[1]
         sum_p, sum_x, sum_y, sum_z = totals
         first = step * per_step
         base = lax.div(first, SLOTS) * LANES + lax.rem(first, SLOTS)
@@ -666,8 +654,21 @@
             sum_z = sum_z + cubic * d_z
         return sum_p, sum_x, sum_y, sum_z
 
+    def far_step(step, carry):
+        added = []
+        for which in range(14):
+            pair = step * 14 + which
+            left = jnp.concatenate([far_rows(2 * pair), far_rows(2 * pair + 1)], axis=1)
+            added.append(lax.dot_general(left, operators[jnp.minimum(pair, used - 1)], NT, preferred_element_type=F32))
+        total = added[0]
+        for value in added[1:]:
+            total = total + value
+        sums[...] += total
+        return carry
+
+    lax.fori_loop(0, STEPS * GROUP // 28, far_step, 0)
     zero = jnp.zeros((SLOTS, LANES), F32)
-    near = lax.fori_loop(0, STEPS, both_step, (zero, zero, zero, zero))
+    near = lax.fori_loop(0, near_steps, both_step, (zero, zero, zero, zero))
 
     staged[5].wait()
     staged[6].wait()
@@ -773,10 +774,18 @@
         made = made * live
         for x in range(block_x):
             piece = made[x * block_y : (x + 1) * block_y]
-            if entry == 0:
-                potential_ref[x] = piece
-            else:
-                field_ref[entry - 1, x] = piece
+            result_ref[entry, x] = piece
+
+
+def part_kernel(result_ref, potential_ref, field_ref, sems):
+    copies = [
+        pltpu.make_async_copy(result_ref.at[0], potential_ref, sems.at[0]),
+        pltpu.make_async_copy(result_ref.at[pl.ds(1, 3)], field_ref, sems.at[1]),
+    ]
+    for copy in copies:
+        copy.start()
+    for copy in copies:
+        copy.wait()
 
 
 def per_device(
@@ -796,21 +805,18 @@
     wide_leaves = wide_x * wide_z * (block_y + 2 * HALO)
     mid_columns = (block_x // 2 + 4) * (block_z // 2 + 4)
     tops = devices // 8
-    anywhere = pl.BlockSpec(memory_space=pl.ANY)
+    anywhere = pl.BlockSpec(memory_space=pltpu.HBM)
     vmem = pl.BlockSpec(memory_space=pltpu.VMEM)
     layout = (triples, none, starts)
     batches = -(-offsets // (6 * PLACED))
     top_rows = (tops + 7) // 8 * 8
     placed = batches * PLACED
     spare = (placed * 6 * terms + 2 * LANES - far_operators.shape[1] + LANES) // LANES * LANES
-    potential, field_out = pl.pallas_call(
+    result = pl.pallas_call(
         lambda *refs: field_kernel(sizes, numbers, layout, *refs),
-        out_shape=(
-            jax.ShapeDtypeStruct((block_x, block_y, column), F32),
-            jax.ShapeDtypeStruct((3, block_x, block_y, column), F32),
-        ),
+        out_shape=pltpu.VMEM((4, block_x, block_y, column), F32),
         in_specs=[anywhere] * 8,
-        out_specs=(vmem, vmem),
+        out_specs=vmem,
         scratch_shapes=[
             pltpu.VMEM(positions.shape, F32),
             pltpu.VMEM(charges.shape, F32),
@@ -838,7 +844,7 @@
             pltpu.VMEM((2 * leaves + 32, padded_terms), F32),
             pltpu.VMEM((LANES, LANES), F32),
             pltpu.SMEM(plan.shape, jnp.int32),
-            pltpu.SMEM((4, LANES), jnp.int32),
+            pltpu.SMEM((4 * LANES,), jnp.int32),
             pltpu.SMEM((triples * 6,), jnp.int32),
             pltpu.SemaphoreType.DMA((8,)),
             pltpu.SemaphoreType.DMA((27,)),
@@ -860,7 +866,18 @@
         jnp.transpose(local_shift, (1, 0, 2)),
         lattice_operator,
     )
-    return potential, field_out
+    return pl.pallas_call(
+        part_kernel,
+        out_shape=(
+            jax.ShapeDtypeStruct((block_x, block_y, column), F32),
+            jax.ShapeDtypeStruct((3, block_x, block_y, column), F32),
+        ),
+        in_specs=[vmem],
+        out_specs=(anywhere, anywhere),
+        scratch_shapes=[pltpu.SemaphoreType.DMA((2,))],
+        compiler_params=pltpu.CompilerParams(vmem_limit_bytes=4 * 1024 * 1024),
+        name="part",
+    )(result)
 
 
 def solution(mesh):

time: 35.5 us -> 29.2 us (0.82)
  Pallas kernels: 32 us -> 28.4 us
  local copies, waits for them, and re-layouts: 2.64 us -> 0 us
    pallas_call x1, Pallas kernels: 32 us -> 27.8 us  [per_device(): pl.pallas_call(lambda *refs: field_kernel(sizes, numbers, layout, *refs),...]
    unnamed x2 -> x0, local copies, waits for them, and re-layouts: 2.64 us -> none
    pallas_call x0 -> x1, Pallas kernels: none -> 0.63 us  [per_device(): pl.pallas_call(part_kernel, out_shape=(jax.ShapeDtypeStruct((block_x, blo...]
where the time goes in v3:
time: 29.2 us; the launch traced here: 29 us
  Pallas kernels  28.4 us (97%)
  between operations  0.64 us (2%)
    pallas_call x1, Pallas kernels, per_device(): pl.pallas_call(lambda *refs: field_kernel(sizes, numbers, layout, *refs),...  27.8 us
    pallas_call x1, Pallas kernels, per_device(): pl.pallas_call(part_kernel, out_shape=(jax.ShapeDtypeStruct((block_x, blo...  0.63 us

profile of v3, /device:TPU:0, one launch (start us, length us, event | category | flops | bytes accessed | tf_op | source)
XLA Modules:
  0.0 29.0 jit_solution(10429345502341516065)
XLA Ops:
  0.6 27.8 %fields.1.result_ref = f32[4,4,4,128]{3,2,1,0:T(4,128)S(1)} custom-call(s32[1344]{0:T(1024)} %constant.2.clone.refs_0_, f32[3,4,4,128]{3,2,1,0:T(4,128)} %refs_1_.1, f32[4,4,128]{2,1,0:T(4,128)} %refs_2_.1, s32[4,4,4]{2,1,0:T(4,128)} %refs_3_.1, bf16[81,8,81]{2,1,0:T(8,128)(2,1)} %bitcast.2, bf16[81,25600]{1,0:T(8,128)(2,1)} %refs_5_.1, ...), custom_call_target="tpu_custom_call" | custom-call | tf_op jit(solution)/shard_map/fields/pallas_call | solution.py:815
  28.4 0.6 %part.1 = (f32[4,4,128]{2,1,0:T(4,128)}, f32[3,4,4,128]{3,2,1,0:T(4,128)}) custom-call(f32[4,4,4,128]{3,2,1,0:T(4,128)S(1)} %fields.1.result_ref), custom_call_target="tpu_custom_call" | custom-call | tf_op jit(solution)/shard_map/part/pallas_call | solution.py:869

commit v4 on v3

--- a/solution.py
+++ b/solution.py
@@ -138,6 +138,9 @@
     receives,
     mid_send,
     mid_receive,
+    arrived,
+    upper_send,
+    upper_receive,
 ):
     block_x, block_y, block_z = sizes
     triples, none, starts = layout
@@ -154,7 +157,16 @@
     barrier = pltpu.get_barrier_semaphore()
 
     def other(step):
+        if devices & (devices - 1) == 0:
+            return (rank + step) & (devices - 1)
         return lax.rem(rank + step, devices)
+
+    def each_other(action):
+        if devices <= 64:
+            for step in range(1, devices):
+                action(step, 0)
+        else:
+            lax.fori_loop(1, devices, action, 0)
 
     staged = [
         pltpu.make_async_copy(positions_hbm, positions, loads.at[0]),
@@ -175,7 +187,7 @@
         )
         return carry
 
-    lax.fori_loop(1, devices, greet, 0)
+    each_other(greet)
 
     lane = lax.broadcasted_iota(jnp.int32, (columns, LANES), 1)
     group = lane // SLOTS
@@ -207,7 +219,6 @@
     targets[...] = own.T
 
     pl.semaphore_wait(barrier, devices - 1)
-    copies = []
     pairs = block_y // 2
 
     def span(move, size, halo):
@@ -217,27 +228,32 @@
             return pl.ds(halo, halo), pl.ds(size + halo, halo)
         return pl.ds(halo, size), pl.ds(halo, size)
 
+    direct, relayed = [], []
     for count in range(27):
         moves = (count // 9 - 1, count // 3 % 3 - 1, count % 3 - 1)
         if moves == (0, 0, 0):
             continue
-        target = tuple(
-            lax.rem(at[axis] + moves[axis] + numbers[axis], numbers[axis]) for axis in range(3)
-        )
         from_x, to_x = span(moves[0], block_x, HALO)
         from_y, to_y = span(moves[1], pairs, 1)
         from_z, to_z = span(moves[2], block_z, HALO)
-        copies.append(
-            pltpu.make_async_remote_copy(
-                src_ref=raw.at[from_y, from_z, from_x],
-                dst_ref=raw.at[to_y, to_z, to_x],
-                send_sem=sends.at[count],
-                recv_sem=receives.at[count],
-                device_id=target,
-                device_id_type=pl.DeviceIdType.MESH,
-            )
+        relay = moves[0] != 0 and moves[1:] != (0, 0)
+        steps = (0 if relay else moves[0],) + moves[1:]
+        target = tuple(
+            lax.rem(at[axis] + steps[axis] + numbers[axis], numbers[axis]) for axis in range(3)
         )
-    for copy in copies:
+        copy = pltpu.make_async_remote_copy(
+            src_ref=raw.at[from_y, from_z, to_x if relay else from_x],
+            dst_ref=raw.at[to_y, to_z, to_x],
+            send_sem=sends.at[count],
+            recv_sem=receives.at[count],
+            device_id=target,
+            device_id_type=pl.DeviceIdType.MESH,
+        )
+        (relayed if relay else direct).append((moves, copy))
+    along_x = [copy for moves, copy in direct if moves[0] != 0]
+    beside = [copy for moves, copy in direct if moves[0] == 0]
+    relayed = [copy for moves, copy in relayed]
+    for copy in along_x + beside:
         copy.start()
 
     partial[pl.ds(terms * 8, partial.shape[0] - terms * 8), :] = jnp.zeros(
@@ -299,27 +315,58 @@
                 lines.append(held[2 * y : 2 * y + 1] + held[2 * y + 1 : 2 * y + 2])
     spare = jnp.zeros((8, LANES - terms), F32)
     own_slot = mids.at[pl.ds(pl.multiple_of(rank * 8, 8), 8)]
-    own_slot[...] = jnp.concatenate([jnp.concatenate(lines, axis=0), spare], axis=1)
-
-    def mid_copy(step):
+    own_mids = jnp.concatenate([jnp.concatenate(lines, axis=0), spare], axis=1)
+    own_slot[...] = own_mids
+
+    mid_copies = []
+    for count in range(27):
+        moves = (count // 9 - 1, count // 3 % 3 - 1, count % 3 - 1)
+        if moves == (0, 0, 0) or any(moves[axis] == -1 and numbers[axis] == 2 for axis in range(3)):
+            continue
+        target = tuple(
+            lax.rem(at[axis] + moves[axis] + numbers[axis], numbers[axis]) for axis in range(3)
+        )
+        mid_copies.append(
+            pltpu.make_async_remote_copy(
+                src_ref=own_slot,
+                dst_ref=own_slot,
+                send_sem=mid_send.at[count],
+                recv_sem=mid_receive.at[count],
+                device_id=target,
+                device_id_type=pl.DeviceIdType.MESH,
+            )
+        )
+    for copy in mid_copies:
+        copy.start()
+    row_eight = lax.broadcasted_iota(jnp.int32, (8, terms), 0)
+    lifted = jnp.zeros((8, terms), F32)
+    for octant in range(8):
+        line = (octant % 2 * 2 + octant // 4) * 2 + octant // 2 % 2
+        found = apply(own_mids, octant_of(shift_rows, octant))
+        lifted = jnp.where(row_eight == line, found, lifted)
+    own_upper = jnp.concatenate([jnp.sum(lifted, axis=0, keepdims=True), spare[:1]], axis=1)
+    upper_slot = arrived.at[rank]
+    upper_slot[...] = own_upper
+
+    def upper_copy(step):
         return pltpu.make_async_remote_copy(
-            src_ref=own_slot,
-            dst_ref=own_slot,
-            send_sem=mid_send.at[step],
-            recv_sem=mid_receive.at[step],
+            src_ref=upper_slot,
+            dst_ref=upper_slot,
+            send_sem=upper_send.at[step],
+            recv_sem=upper_receive.at[step],
             device_id=other(step),
             device_id_type=pl.DeviceIdType.LOGICAL,
         )
 
-    def send_mid(step, carry):
-        mid_copy(step).start()
+    def send_upper(step, carry):
+        upper_copy(step).start()
         return carry
 
-    def wait_mid(step, carry):
-        mid_copy(step).wait()
+    def wait_upper(step, carry):
+        upper_copy(step).wait()
         return carry
 
-    lax.fori_loop(1, devices, send_mid, 0)
+    each_other(send_upper)
 
     strides = (numbers[1] * numbers[2], numbers[2], 1)
     top_sizes = tuple(number // 2 for number in numbers)
@@ -390,12 +437,16 @@
         return carry
 
     used = operators.shape[0]
-    lax.fori_loop(0, used // PLACED, place, 0)
+    batches = used // PLACED
+    lax.fori_loop(0, batches // 2, place, 0)
+    for copy in along_x:
+        copy.wait()
+    for copy in relayed:
+        copy.start()
+    lax.fori_loop(batches // 2, batches, place, 0)
     for row in range(used * 6, triples * 3):
         reach_of(row)
 
-    for copy in copies:
-        copy.wait()
     guard = 8
 
     def clear(ref):
@@ -413,56 +464,6 @@
     def halved(value):
         upper = value.astype(BF16).astype(F32)
         return upper, (value - upper).astype(BF16).astype(F32)
-
-    def widen(z, carry):
-        for x in range(wide_x):
-            column = jnp.concatenate([raw[pair, z, x] for pair in range(pairs + 2)], axis=0)
-            wide[pl.ds(pl.multiple_of(guard + (z * wide_x + x) * rows_y, 8), rows_y), :] = column
-        return carry
-
-    lax.fori_loop(0, wide_z, widen, 0)
-
-    def window(tile, carry):
-        start = pl.multiple_of(guard + tile * LANES, 8)
-        turned = wide[pl.ds(start, LANES), :].T
-        found = moments(
-            turned[:SLOTS], turned[SLOTS : 2 * SLOTS], turned[2 * SLOTS : 3 * SLOTS], turned[3 * SLOTS :]
-        )
-        for kind, value in enumerate(third(found)):
-            upper, lower = halved(value)
-            moments_high[kind, pl.ds(start, LANES), :] = upper
-            moments_low[kind, pl.ds(start, LANES), :] = lower
-        return carry
-
-    lax.fori_loop(0, wide_x * wide_z * rows_y // LANES, window, 0, unroll=2)
-
-    near_shifts = [(x, y, z) for x in (-1, 0, 1) for y in (-1, 0, 1) for z in (-1, 0, 1)]
-    lane8 = lax.broadcasted_iota(jnp.int32, (8, LANES), 1)
-    group8 = lane8 // SLOTS
-
-    def shifted(shift):
-        moved = jnp.where(
-            group8 == 0,
-            float(shift[0]),
-            jnp.where(group8 == 1, float(shift[1]), jnp.where(group8 == 2, float(shift[2]), 0.0)),
-        )
-        found = []
-        for z in range(block_z):
-            for x in range(0, block_x, 2):
-                spot = (z + HALO + shift[2]) * wide_x + x + HALO + shift[0]
-                low = guard + spot * rows_y + HALO + shift[1]
-                high = low + rows_y - block_y
-                held = jnp.where(row8 < block_y, wide[low : low + 8, :], wide[high : high + 8, :])
-                found.append(held + moved)
-        return found
-
-    for pair in range((len(near_shifts) + 1) // 2):
-        first = shifted(near_shifts[2 * pair])
-        if 2 * pair + 1 < len(near_shifts):
-            second = shifted(near_shifts[2 * pair + 1])
-        else:
-            second = [jnp.where(group8 < 3, value, 0.0) for value in first]
-        sources[pair * LANES : (pair + 1) * LANES, :] = jnp.concatenate(first + second, axis=0).T
 
     odd_line = row8 % 2 == 1
     zero8 = jnp.zeros((8, LANES), F32)
@@ -474,32 +475,8 @@
             return jnp.where(odd_line, 0.0, page)
         return page
 
-    def fill_pages(z, carry):
-        for shift in range(-3, 4):
-            spot = ((shift + 3) * wide_z + z) * starts
-            for kind in range(3):
-                made = []
-                for x in range(wide_x):
-                    start = guard + (z * wide_x + x) * rows_y + HALO + shift
-                    page = jnp.where(
-                        row8 < block_y,
-                        moments_high[kind, pl.ds(start, 8), :],
-                        moments_low[kind, pl.ds(start - block_y, 8), :],
-                    )
-                    made.append(parity(page, shift))
-                listed = [(x, made[x], made[x + 1]) for x in range(wide_x - 1)]
-                listed += [(7, zero8, made[0]), (9, zero8, made[2])]
-                listed += [(8, made[5], zero8), (10, made[7], zero8)]
-                for entry, low, high in listed:
-                    pages[kind, spot + entry] = jnp.concatenate([low, high], axis=0).astype(BF16)
-        return carry
-
-    lax.fori_loop(0, wide_z, fill_pages, 0)
-    for kind in range(6):
-        for entry in range(pages.shape[1] - none):
-            pages[kind, none + entry] = jnp.zeros((16, LANES), BF16)
-
-    lax.fori_loop(1, devices, wait_mid, 0)
+    for copy in mid_copies:
+        copy.wait()
     mid_x, mid_z = block_x // 2 + 4, block_z // 2 + 4
     around = []
     for count in range(27):
@@ -544,11 +521,8 @@
 
     lax.fori_loop(0, mid_z, fill_mids, 0)
 
-    raised = jnp.zeros((devices, terms), F32)
-    for octant in range(8):
-        line = (octant % 2 * 2 + octant // 4) * 2 + octant // 2 % 2
-        raised = raised + apply(mids[pl.ds(line, devices, stride=8), :], octant_of(shift_rows, octant))
-    raised = jnp.concatenate([raised, jnp.zeros((devices, LANES - terms), F32)], axis=1)
+    each_other(wait_upper)
+    raised = arrived[:, 0, :]
     rank_row = lax.broadcasted_iota(jnp.int32, (devices, terms), 0)
     rank_octant = (
         4 * (rank_row // strides[0] % 2) + 2 * (rank_row // strides[1] % 2) + rank_row % 2
@@ -593,6 +567,83 @@
         upper_pages[kind, devices] = jnp.zeros((16, LANES), BF16)
         upper_pages[kind, devices + 1 + tops] = jnp.zeros((16, LANES), BF16)
 
+    for copy in beside + relayed:
+        copy.wait()
+    def widen(z, carry):
+        for x in range(wide_x):
+            column = jnp.concatenate([raw[pair, z, x] for pair in range(pairs + 2)], axis=0)
+            wide[pl.ds(pl.multiple_of(guard + (z * wide_x + x) * rows_y, 8), rows_y), :] = column
+        return carry
+
+    lax.fori_loop(0, wide_z, widen, 0)
+
+    def window(tile, carry):
+        start = pl.multiple_of(guard + tile * LANES, 8)
+        turned = wide[pl.ds(start, LANES), :].T
+        found = moments(
+            turned[:SLOTS], turned[SLOTS : 2 * SLOTS], turned[2 * SLOTS : 3 * SLOTS], turned[3 * SLOTS :]
+        )
+        for kind, value in enumerate(third(found)):
+            upper, lower = halved(value)
+            moments_high[kind, pl.ds(start, LANES), :] = upper
+            moments_low[kind, pl.ds(start, LANES), :] = lower
+        return carry
+
+    lax.fori_loop(0, wide_x * wide_z * rows_y // LANES, window, 0, unroll=4)
+
+    near_shifts = [(x, y, z) for x in (-1, 0, 1) for y in (-1, 0, 1) for z in (-1, 0, 1)]
+    lane8 = lax.broadcasted_iota(jnp.int32, (8, LANES), 1)
+    group8 = lane8 // SLOTS
+
+    def shifted(shift):
+        moved = jnp.where(
+            group8 == 0,
+            float(shift[0]),
+            jnp.where(group8 == 1, float(shift[1]), jnp.where(group8 == 2, float(shift[2]), 0.0)),
+        )
+        found = []
+        for z in range(block_z):
+            for x in range(0, block_x, 2):
+                spot = (z + HALO + shift[2]) * wide_x + x + HALO + shift[0]
+                low = guard + spot * rows_y + HALO + shift[1]
+                high = low + rows_y - block_y
+                held = jnp.where(row8 < block_y, wide[low : low + 8, :], wide[high : high + 8, :])
+                found.append(held + moved)
+        return found
+
+    for pair in range((len(near_shifts) + 1) // 2):
+        first = shifted(near_shifts[2 * pair])
+        if 2 * pair + 1 < len(near_shifts):
+            second = shifted(near_shifts[2 * pair + 1])
+        else:
+            second = [jnp.where(group8 < 3, value, 0.0) for value in first]
+        sources[pair * LANES : (pair + 1) * LANES, :] = jnp.concatenate(first + second, axis=0).T
+
+    def fill_pages(z, carry):
+        for shift in range(-3, 4):
+            spot = ((shift + 3) * wide_z + z) * starts
+            for kind in range(3):
+                made = []
+                for x in range(wide_x):
+                    start = guard + (z * wide_x + x) * rows_y + HALO + shift
+                    page = jnp.where(
+                        row8 < block_y,
+                        moments_high[kind, pl.ds(start, 8), :],
+                        moments_low[kind, pl.ds(start - block_y, 8), :],
+                    )
+                    made.append(parity(page, shift))
+                listed = [(x, made[x], made[x + 1]) for x in range(wide_x - 1)]
+                listed += [(7, zero8, made[0]), (9, zero8, made[2])]
+                listed += [(8, made[5], zero8), (10, made[7], zero8)]
+                for entry, low, high in listed:
+                    pages[kind, spot + entry] = jnp.concatenate([low, high], axis=0).astype(BF16)
+        return carry
+
+    lax.fori_loop(0, wide_z, fill_pages, 0)
+    for kind in range(6):
+        for entry in range(pages.shape[1] - none):
+            pages[kind, none + entry] = jnp.zeros((16, LANES), BF16)
+
     lane16 = lax.broadcasted_iota(jnp.int32, (16, LANES), 1)
     first_part = lane16 < terms
     second_part = lane16 < 2 * terms - LANES
@@ -630,14 +681,13 @@
 
     total_rows = 2 * leaves + 32
     sums[...] = jnp.zeros(sums.shape, F32)
-    near_steps = sources.shape[0] // LANES
-    per_step = SLOTS
-
-    def both_step(step, totals):
+    near_steps = sources.shape[0] // LANES // 2
+
+    def near_step(step, totals):
         sum_p, sum_x, sum_y, sum_z = totals
-        first = step * per_step
-        base = lax.div(first, SLOTS) * LANES + lax.rem(first, SLOTS)
-        for line in range(per_step):
+        for row in range(2 * SLOTS):
+            base = step * (2 * LANES) + row // SLOTS * LANES
+            line = row % SLOTS
             s_x = sources[pl.ds(base + line, 1), :]
             s_y = sources[pl.ds(base + line + SLOTS, 1), :]
             s_z = sources[pl.ds(base + line + 2 * SLOTS, 1), :]
@@ -668,7 +718,7 @@
 
     lax.fori_loop(0, STEPS * GROUP // 28, far_step, 0)
     zero = jnp.zeros((SLOTS, LANES), F32)
-    near = lax.fori_loop(0, near_steps, both_step, (zero, zero, zero, zero))
+    near = lax.fori_loop(0, near_steps, near_step, (zero, zero, zero, zero))
 
     staged[5].wait()
     staged[6].wait()
@@ -849,6 +899,9 @@
             pltpu.SemaphoreType.DMA((8,)),
             pltpu.SemaphoreType.DMA((27,)),
             pltpu.SemaphoreType.DMA((27,)),
+            pltpu.SemaphoreType.DMA((27,)),
+            pltpu.SemaphoreType.DMA((27,)),
+            pltpu.VMEM((devices, 1, LANES), F32),
             pltpu.SemaphoreType.DMA((devices,)),
             pltpu.SemaphoreType.DMA((devices,)),
         ],

time: 29.2 us -> 28.3 us (0.969)
  Pallas kernels: 28.4 us -> 27.5 us
    pallas_call x1, Pallas kernels: 27.8 us -> 26.9 us  [per_device(): pl.pallas_call(lambda *refs: field_kernel(sizes, numbers, layout, *refs),...]
where the time goes in v4:
time: 28.3 us; the launch traced here: 28.1 us
  Pallas kernels  27.5 us (97%)
  between operations  0.64 us (2%)
    pallas_call x1, Pallas kernels, per_device(): pl.pallas_call(lambda *refs: field_kernel(sizes, numbers, layout, *refs),...  26.9 us
    pallas_call x1, Pallas kernels, per_device(): pl.pallas_call(part_kernel, out_shape=(jax.ShapeDtypeStruct((block_x, blo...  0.63 us

profile of v4, /device:TPU:0, one launch (start us, length us, event | category | flops | bytes accessed | tf_op | source)
XLA Modules:
  0.0 28.1 jit_solution(13343502964595547926)
XLA Ops:
  0.6 26.9 %fields.1.result_ref = f32[4,4,4,128]{3,2,1,0:T(4,128)S(1)} custom-call(s32[1344]{0:T(1024)} %constant.2.clone.refs_0_, f32[3,4,4,128]{3,2,1,0:T(4,128)} %refs_1_.1, f32[4,4,128]{2,1,0:T(4,128)} %refs_2_.1, s32[4,4,4]{2,1,0:T(4,128)} %refs_3_.1, bf16[81,8,81]{2,1,0:T(8,128)(2,1)} %bitcast.2, bf16[81,25600]{1,0:T(8,128)(2,1)} %refs_5_.1, ...), custom_call_target="tpu_custom_call" | custom-call | tf_op jit(solution)/shard_map/fields/pallas_call | solution.py:865
  27.5 0.6 %part.1 = (f32[4,4,128]{2,1,0:T(4,128)}, f32[3,4,4,128]{3,2,1,0:T(4,128)}) custom-call(f32[4,4,4,128]{3,2,1,0:T(4,128)S(1)} %fields.1.result_ref), custom_call_target="tpu_custom_call" | custom-call | tf_op jit(solution)/shard_map/part/pallas_call | solution.py:922

commit v5 on v4

--- a/solution.py
+++ b/solution.py
@@ -250,6 +250,8 @@
             device_id_type=pl.DeviceIdType.MESH,
         )
         (relayed if relay else direct).append((moves, copy))
+    direct.sort(key=lambda held: held[0][2] == 0)
+    relayed.sort(key=lambda held: held[0][2] == 0)
     along_x = [copy for moves, copy in direct if moves[0] != 0]
     beside = [copy for moves, copy in direct if moves[0] == 0]
     relayed = [copy for moves, copy in relayed]
@@ -475,6 +477,13 @@
             return jnp.where(odd_line, 0.0, page)
         return page
 
+    for kind in range(6):
+        for entry in range(pages.shape[1] - none):
+            pages[kind, none + entry] = jnp.zeros((16, LANES), BF16)
+    staged[5].wait()
+    staged[6].wait()
+    rows_from(down_raw, down_rows)
+    sums[...] = jnp.zeros(sums.shape, F32)
     for copy in mid_copies:
         copy.wait()
     mid_x, mid_z = block_x // 2 + 4, block_z // 2 + 4
@@ -640,9 +649,6 @@
         return carry
 
     lax.fori_loop(0, wide_z, fill_pages, 0)
-    for kind in range(6):
-        for entry in range(pages.shape[1] - none):
-            pages[kind, none + entry] = jnp.zeros((16, LANES), BF16)
 
     lane16 = lax.broadcasted_iota(jnp.int32, (16, LANES), 1)
     first_part = lane16 < terms
@@ -680,7 +686,6 @@
         return jnp.concatenate(found, axis=0)
 
     total_rows = 2 * leaves + 32
-    sums[...] = jnp.zeros(sums.shape, F32)
     near_steps = sources.shape[0] // LANES // 2
 
     def near_step(step, totals):
@@ -720,9 +725,6 @@
     zero = jnp.zeros((SLOTS, LANES), F32)
     near = lax.fori_loop(0, near_steps, near_step, (zero, zero, zero, zero))
 
-    staged[5].wait()
-    staged[6].wait()
-    rows_from(down_raw, down_rows)
     first = 2 * leaves + 16
     held = sums[first : first + 8, :terms]
     far_upper = held[0:1] + held[1:2]

time: 28.3 us -> 28.2 us (level)
  no operation moved by 1% of the time
where the time goes in v5:
time: 28.2 us; the launch traced here: 28.1 us
  Pallas kernels  27.4 us (97%)
  between operations  0.64 us (2%)
    pallas_call x1, Pallas kernels, per_device(): pl.pallas_call(lambda *refs: field_kernel(sizes, numbers, layout, *refs),...  26.8 us
    pallas_call x1, Pallas kernels, per_device(): pl.pallas_call(part_kernel, out_shape=(jax.ShapeDtypeStruct((block_x, blo...  0.63 us

profile of v5, /device:TPU:0, one launch (start us, length us, event | category | flops | bytes accessed | tf_op | source)
XLA Modules:
  0.0 28.1 jit_solution(9770859811805849647)
XLA Ops:
  0.6 26.8 %fields.1.result_ref = f32[4,4,4,128]{3,2,1,0:T(4,128)S(1)} custom-call(s32[1344]{0:T(1024)} %constant.2.clone.refs_0_, f32[3,4,4,128]{3,2,1,0:T(4,128)} %refs_1_.1, f32[4,4,128]{2,1,0:T(4,128)} %refs_2_.1, s32[4,4,4]{2,1,0:T(4,128)} %refs_3_.1, bf16[81,8,81]{2,1,0:T(8,128)(2,1)} %bitcast.2, bf16[81,25600]{1,0:T(8,128)(2,1)} %refs_5_.1, ...), custom_call_target="tpu_custom_call" | custom-call | tf_op jit(solution)/shard_map/fields/pallas_call | solution.py:867
  27.5 0.6 %part.1 = (f32[4,4,128]{2,1,0:T(4,128)}, f32[3,4,4,128]{3,2,1,0:T(4,128)}) custom-call(f32[4,4,4,128]{3,2,1,0:T(4,128)S(1)} %fields.1.result_ref), custom_call_target="tpu_custom_call" | custom-call | tf_op jit(solution)/shard_map/part/pallas_call | solution.py:924
